TPU v7x, 768 devices: a whole 4x8x12 slice. The times are simulated.
768 devices in a mesh: shard: 24 (over z, y_lo), replica: 32 (over x, y_hi, core).
Axes of the slice: x: 4, y: 8 (y_hi: 4, y_lo: 2; y = y_hi * 2 + y_lo), z: 12, core: 2. Of those that a mesh axis runs over, the one named last changes fastest.
Arguments:
- atom_feats: bfloat16 [49152, 9, 128], P(('shard', 'replica')), may hold values from -6 to 6
- cotangent: bfloat16 [49152, 9, 128], P(('shard', 'replica')), may hold values from -6 to 6
- frames: bfloat16 [9, 9, 196608], P(None, None, ('shard', 'replica')), may hold values from -2 to 2
- radial: bfloat16 [196608, 128], P(('shard', 'replica')), may hold values from 0.19921875 to 2
- edge_source: int32 [196608], P(('shard', 'replica')), may hold values from 0 to 63
- edge_target: int32 [196608], P(('shard', 'replica')), may hold values from 0 to 63
- edge_valid: int32 [196608], P(('shard', 'replica')), may hold values 0 or 1
- atom_types: int32 [49152], P(('shard', 'replica')), may hold values from 0 to 99
- dataset: int32 [768], P(('shard', 'replica')), may hold values from 0 to 4
- type_table: float32 [100, 128], replicated, may hold values from -6 to 6
- dataset_table: float32 [5, 128], replicated, may hold values from -6 to 6
- router_weight: float32 [128, 28], replicated, may hold values from -1.5 to 1.5
- experts: bfloat16 [28, 384, 384], P(None, 'shard'), may hold values from -3 to 3
Outputs:
- updated: bfloat16 [49152, 9, 128], P(('shard', 'replica'))
- feats_grad: float32 [49152, 9, 128], P(('shard', 'replica'))
- expert_grad: float32 [28, 384, 384], P(None, 'shard')
Inputs may be any that keep to these rules, and one draw needn't show every extreme that they name: `edge_source`: indices of atoms within the edge's own system. `edge_target`: indices of atoms within the edge's own system.
All inputs are finite; a program needn't handle non-finite values. No bound on the sum of `edge_valid` on one device may be relied on, other than what follows from the above.
Results may differ from a plain program's by a relative error of at most 0.011.
Values may be sent and summed in bfloat16 or wider, within the bound.
No kernel may reach another device: no remote copies, remote signals or barrier semaphores. Data moves between devices by JAX's collectives and lax.ppermute only.
A program may use at most 64 MiB of HBM per device.

v0:
```python
import math

import jax
import jax.numpy as jnp
from jax import lax
from jax.sharding import PartitionSpec as P


def sent_to_all(shard, axis):
    devices = lax.axis_size(axis)
    return lax.all_to_all(
        jnp.broadcast_to(shard[None], (devices, *shard.shape)), axis, 0, 0, tiled=True
    )


def laid_out(tiles, dim):
    shape = list(tiles.shape[1:])
    shape[dim] *= tiles.shape[0]
    return jnp.moveaxis(tiles, 0, dim).reshape(shape)


def gather_directly(shard, axis, dim):
    tiles = sent_to_all(shard, axis)
    return laid_out(tiles, dim)


def filled_up(lines, devices):
    spare = -lines.shape[0] % devices
    if not spare:
        return lines
    return jnp.concatenate([lines, jnp.zeros((spare, *lines.shape[1:]), lines.dtype)])


def sum_by_parts(shard, axis):
    lines = shard.reshape(-1, *shard.shape[1:][-1:])
    padded = filled_up(lines, lax.axis_size(axis))
    own = lax.psum_scatter(padded, axis, scatter_dimension=0, tiled=True)
    whole = lax.all_gather(own, axis, axis=0, tiled=True)
    return whole[: len(lines)].reshape(shard.shape)


def system_mix(type_rows, dataset_one, type_table, dataset_table, router_weight):
    table_size = type_table.shape[0]
    onehot = (type_rows[:, None] == jnp.arange(table_size, dtype=jnp.int32)[None, :]).astype(
        jnp.float32
    )
    counts = jnp.sum(onehot, axis=0)
    embed = jnp.dot(counts, type_table, precision=lax.Precision.HIGHEST) / type_rows.shape[0]
    pick = (
        dataset_one[:, None] == jnp.arange(dataset_table.shape[0], dtype=jnp.int32)[None, :]
    ).astype(jnp.float32)
    embed = embed + jnp.dot(pick, dataset_table, precision=lax.Precision.HIGHEST)[0]
    soft = jax.nn.softplus(jnp.dot(embed, router_weight, precision=lax.Precision.HIGHEST))
    return soft / jnp.sum(soft)


def edge_layer(feats32, merged32, frames, radial, source, target, valid):
    atom_count, components, channels = feats32.shape
    edge_count = source.shape[0]
    top_degree = math.isqrt(components) - 1
    feats = feats32.astype(jnp.bfloat16)
    merged = merged32.astype(jnp.bfloat16)
    gathered = jnp.take(feats, source, axis=0)
    rotated = jnp.einsum(
        "ije,ejc->eic", frames.astype(jnp.float32), gathered.astype(jnp.float32)
    ).astype(jnp.bfloat16)
    zero_rows = [degree * degree + degree for degree in range(top_degree + 1)]
    zero_band = jnp.concatenate(
        [rotated[:, row : row + 1, :] for row in zero_rows], axis=1
    ).reshape(edge_count, -1)
    mixed_band = jnp.dot(zero_band, merged, preferred_element_type=jnp.float32).reshape(
        edge_count, top_degree + 1, channels
    )
    columns = []
    for column in range(components):
        if column in zero_rows:
            columns.append(mixed_band[:, zero_rows.index(column), :])
        else:
            columns.append(rotated[:, column, :].astype(jnp.float32))
    combined = jnp.stack(columns, axis=1)
    message = (combined * radial.astype(jnp.float32)[:, None, :]).astype(jnp.bfloat16)
    unrotated = jnp.einsum(
        "jie,ejc->eic", frames.astype(jnp.float32), message.astype(jnp.float32)
    ).astype(jnp.bfloat16)
    incidence = (
        (target[None, :] == jnp.arange(atom_count, dtype=jnp.int32)[:, None]) & (valid[None, :] > 0)
    ).astype(jnp.bfloat16)
    summed = jnp.dot(
        incidence, unrotated.reshape(edge_count, -1), preferred_element_type=jnp.float32
    )
    return feats32 + summed.reshape(atom_count, components, channels) * (atom_count / edge_count)


def add_system(total, pair):
    mix_row, rows = pair
    term = lax.optimization_barrier((mix_row[:, None, None] * rows[None]).astype(jnp.bfloat16))
    return (total + term.astype(jnp.float32), None)


def shards(
    atom_feats,
    cotangent,
    frames,
    radial,
    edge_source,
    edge_target,
    edge_valid,
    atom_types,
    dataset,
    type_table,
    dataset_table,
    router_weight,
    experts,
):
    group = lax.axis_size("shard")
    row_block = experts.shape[1]
    row_total = row_block * group
    mixture = system_mix(atom_types, dataset, type_table, dataset_table, router_weight)
    group_mixtures = gather_directly(mixture[None, :], "shard", 0)
    row_shares = jnp.einsum(
        "sk,krc->src", group_mixtures, experts.astype(jnp.float32), precision=lax.Precision.HIGHEST
    ).astype(jnp.bfloat16)
    merged = lax.all_to_all(row_shares, "shard", split_axis=0, concat_axis=1, tiled=True).reshape(
        row_total, -1
    )
    merged32 = lax.optimization_barrier(merged).astype(jnp.float32)

    def local(feats32, weight32):
        return edge_layer(feats32, weight32, frames, radial, edge_source, edge_target, edge_valid)

    result, pullback = jax.vjp(local, atom_feats.astype(jnp.float32), merged32)
    feats_grad, weight_grad = pullback(cotangent.astype(jnp.float32))
    back_mixtures = gather_directly(mixture[None, :], "shard", 0)
    received = lax.all_to_all(
        weight_grad.reshape(group, row_block, -1).astype(jnp.bfloat16),
        "shard",
        split_axis=0,
        concat_axis=0,
        tiled=True,
    ).astype(jnp.float32)
    start = jnp.zeros(experts.shape, jnp.float32)
    shard_sum, unused = lax.scan(add_system, start, (back_mixtures, received))
    expert_grad = sum_by_parts(shard_sum, "replica")
    return (result.astype(jnp.bfloat16), feats_grad, expert_grad)


def solution(mesh):
    in_specs = (
        P(("shard", "replica"), None, None),
        P(("shard", "replica"), None, None),
        P(None, None, ("shard", "replica")),
        P(("shard", "replica"), None),
        P(("shard", "replica")),
        P(("shard", "replica")),
        P(("shard", "replica")),
        P(("shard", "replica")),
        P(("shard", "replica")),
        P(),
        P(),
        P(),
        P(None, "shard", None),
    )
    out_specs = (
        P(("shard", "replica"), None, None),
        P(("shard", "replica"), None, None),
        P(None, "shard", None),
    )
    return jax.shard_map(shards, mesh=mesh, in_specs=in_specs, out_specs=out_specs, check_vma=False)
```

profile of v0, /device:TPU:1, one launch (start us, length us, event | category | flops | bytes accessed | tf_op | source)
XLA Modules:
  0.0 254.5 jit_solution(10592647568989537782)
XLA Ops:
  2.9 1.0 fusion.8
  3.9 1.5 fusion.52
  6.6 16.9 %all-to-all-start = ((f32[24,1,28]{2,1,0:T(1,128)}), f32[24,1,28]{2,1,0:T(1,128)S(1)}, u32[]{:S(2)}, u32[]{:S(2)}) async-start(f32[24,1,28]{2,1,0:T(1,128)} %broadcast_in_dim.22), calls=%async_computation | async-start | bytes 24576 | tf_op jit(solution)/shard_map/all_to_all | solution.py:11
  24.9 1.9 copy.97
  26.8 2.8 %gather_fusion = bf16[256,9,128]{2,0,1:T(8,128)(2,1)S(1)} fusion(bf16[64,9,128]{2,0,1:T(8,128)(2,1)S(1)} %copy-done.1, s32[1024]{0:T(1024)S(1)} %pad_clamp_fusion), kind=kCustom, calls=%fused_computation | custom fusion | bytes 1180672 | tf_op jit(solution)/shard_map/jvp(jit(_take))/gather | solution.py:63
  30.4 1.6 slice_convert_fusion
  33.3 1.0 copy.110
  34.3 0.9 convert_element_type.132
  35.2 1.4 fusion.53
  37.3 1.0 fusion.55
  38.3 10.0 %all-to-all-start.2 = ((bf16[24,16,384]{2,1,0:T(8,128)(2,1)}), bf16[24,16,384]{2,1,0:T(8,128)(2,1)S(1)}, u32[]{:S(2)}, u32[]{:S(2)}) async-start(bf16[24,16,384]{2,1,0:T(8,128)(2,1)} %bitcast.25), calls=%async_computation.2 | async-start | bytes 589824 | tf_op jit(solution)/shard_map/all_to_all | solution.py:134
  48.4 1.9 copy.106
  50.4 1.3 dynamic-slice.4
  52.3 1.5 fusion.49
  54.9 8.2 %all-to-all-done.2 = bf16[24,16,384]{2,1,0:T(8,128)(2,1)S(1)} async-done(((bf16[24,16,384]{2,1,0:T(8,128)(2,1)}), bf16[24,16,384]{2,1,0:T(8,128)(2,1)S(1)}, u32[]{:S(2)}, u32[]{:S(2)}) %all-to-all-start.2) | async-done | bytes 294944 | tf_op jit(solution)/shard_map/all_to_all | solution.py:134
  63.1 5.7 %all-to-all-start.1 = ((bf16[24,16,384]{2,1,0:T(8,128)(2,1)}), bf16[24,16,384]{2,1,0:T(8,128)(2,1)S(1)}, u32[]{:S(2)}, u32[]{:S(2)}) async-start(bf16[24,16,384]{2,1,0:T(8,128)(2,1)} %copy.100), calls=%async_computation.1 | async-start | bytes 589824 | tf_op jit(solution)/shard_map/all_to_all | solution.py:123
  68.8 0.9 convert_element_type.147
  69.6 26.3 %while.11 = (s32[]{:T(128)}, f32[28,16,384]{2,1,0:T(8,128)S(1)}, f32[24,28]{1,0:T(8,128)S(1)}, f32[24,16,384]{2,1,0:T(8,128)}, s32[]{:T(128)}, /*index=5*/s32[]{:T(128)}) while((s32[]{:T(128)}, f32[28,16,384]{2,1,0:T(8,128)S(1)}, f32[24,28]{1,0:T(8,128)S(1)}, f32[24,16,384]{2,1,0:T(8,128)}, s32[]{:T(128)}, ...), condition=%wide.region_4.5_spmd.clone, body=%wide.region_3.4_spmd.clone.sunk | while | flops 860163 | bytes 2138535 | solution.py:142
  96.0 77.4 %fusion = f32[16,384]{1,0:T(8,128)S(1)} fusion(f32[448,384]{1,0:T(8,128)S(1)} %bitcast.94), kind=kCustom, calls=%all-reduce-scatter | all-reduce-scatter fusion | flops 196609 | bytes 716800
  173.4 1.9 collective-permute-start
  175.3 1.3 collective-permute-start.1
  176.6 1.9 collective-permute-start.2
  178.5 2.1 collective-permute-start.3
  182.2 3.1 %stack.2 = f32[256,9,128]{2,1,0:T(8,128)S(1)} concatenate(f32[256,1,128]{2,1,0:T(1,128)} %bitcast.106, f32[256,1,128]{2,1,0:T(1,128)} %get-tuple-element.62, f32[256,1,128]{2,1,0:T(1,128)} %bitcast.105, f32[256,1,128]{2,1,0:T(1,128)} %get-tuple-element.61, f32[256,1,128]{2,1,0:T(1,128)S(1)} %copy-done.9, f32[256,1,128]{2,1,0:T(1,128)S(1)} %copy-done.8, f32[256,1,128]{2,1,0:T(1,128)} %bitcast.104, ...), dimensions={1} | concatenate | bytes 2359296 | tf_op jit(solution)/shard_map/jvp()/stack | solution.py:80
  185.3 2.6 %fusion.2 = bf16[256,9,128]{2,1,0:T(8,128)(2,1)} fusion(bf16[9,9,256]{0,1,2:T(8,128)(2,1)} %copy.106, f32[256,9,128]{2,1,0:T(8,128)S(1)} %stack.2, f32[256,128]{1,0:T(8,128)S(1)} %convert_element_type.132), kind=kOutput, calls=%fused_computation.14 | convolution fusion | flops 6193152 | bytes 1942016 | tf_op jit(solution)/shard_map/jvp(jie,ejc->eic)/dot_general | solution.py:82
  188.0 1.8 copy.107
  189.8 1.0 fusion.5
  192.0 3.3 %fusion.3 = bf16[256,9,128]{2,1,0:T(8,128)(2,1)S(1)} fusion(bf16[9,9,256]{0,1,2:T(8,128)(2,1)S(1)} %copy-done.2, bf16[256,1,128]{2,1,0:T(2,128)(2,1)} %copy.126, bf16[256,1,128]{2,1,0:T(2,128)(2,1)S(1)} %copy.125, bf16[256,1,128]{2,1,0:T(2,128)(2,1)S(1)} %copy.124, bf16[256,1,128]{2,1,0:T(2,128)(2,1)S(1)} %copy-done.12, ...), kind=kOutput, calls=%fused_computation.15 | convolution fusion | flops 10911744 | bytes 1221120 | tf_op jit(solution)/shard_map/transpose(jvp(ije,ejc->eic))/dot_general | solution.py:64
  195.4 9.3 %scatter_fusion = bf16[64,9,128]{2,1,0:T(8,128)(2,1)S(1)} fusion(bf16[64,9,128]{2,1,0:T(8,128)(2,1)S(1)} %broadcast_in_dim.23, s32[256]{0:T(256)S(1)} %compare_select_fusion, bf16[256,9,128]{2,1,0:T(8,128)(2,1)S(1)} %fusion.3), kind=kCustom, calls=%fused_computation.1 | custom fusion | flops 294912 | bytes 1770496 | tf_op jit(solution)/shard_map/transpose(jvp(jit(_take)))/scatter-add | solution.py:63
  205.5 1.9 concatenate.4
  207.4 46.2 %all-gather = f32[32,14,384]{2,1,0:T(8,128)S(1)} all-gather(f32[1,14,384]{2,1,0:T(8,128)S(1)} %dynamic-slice_bitcast_fusion.2), channel_id=1, replica_groups=mesh['shard'=24,'replica'=32] {'replica'}, dimensions={0}, use_global_device_ids=true | all-gather | bytes 709632 | tf_op jit(solution)/shard_map/all_gather | solution.py:38
  253.6 0.9 reshape.80
  (171 shorter events, 37.1 us)
Async XLA Ops:
  0.6 53.1 %copy-start = (bf16[28,16,384]{2,1,0:T(8,128)(2,1)S(1)}, bf16[28,16,384]{2,1,0:T(8,128)(2,1)}, u32[]{:S(2)}) copy-start(bf16[28,16,384]{2,1,0:T(8,128)(2,1)} %param.27) | copy-start | bytes 1032196
  0.6 26.2 %copy-start.1 = (bf16[64,9,128]{2,0,1:T(8,128)(2,1)S(1)}, bf16[64,9,128]{2,0,1:T(8,128)(2,1)}, u32[]{:S(2)}) copy-start(bf16[64,9,128]{2,0,1:T(8,128)(2,1)} %param.15) | copy-start | bytes 442372
  6.6 31.7 %all-to-all-start = ((f32[24,1,28]{2,1,0:T(1,128)}), f32[24,1,28]{2,1,0:T(1,128)S(1)}, u32[]{:S(2)}, u32[]{:S(2)}) async-start(f32[24,1,28]{2,1,0:T(1,128)} %broadcast_in_dim.22), calls=%async_computation | async-start | bytes 24576 | tf_op jit(solution)/shard_map/all_to_all | solution.py:11
  30.3 2.3 copy-start.17
  30.3 2.3 copy-start.4
  30.4 2.3 copy-start.15
  35.2 1.6 copy-start.16
  36.6 11.8 %copy-start.10 = (bf16[9,9,256]{2,1,0:T(8,128)(2,1)S(1)}, bf16[9,9,256]{2,1,0:T(8,128)(2,1)}, u32[]{:S(2)}) copy-start(bf16[9,9,256]{2,1,0:T(8,128)(2,1)} %param.17) | copy-start | bytes 124420
  36.8 15.5 %copy-start.3 = (bf16[256,9,128]{2,1,0:T(8,128)(2,1)S(1)}, bf16[256,9,128]{2,1,0:T(8,128)(2,1)}, u32[]{:S(2)}) copy-start(bf16[256,9,128]{2,1,0:T(8,128)(2,1)} %get-tuple-element.74) | copy-start | bytes 1769476
  38.3 24.8 %all-to-all-start.2 = ((bf16[24,16,384]{2,1,0:T(8,128)(2,1)}), bf16[24,16,384]{2,1,0:T(8,128)(2,1)S(1)}, u32[]{:S(2)}, u32[]{:S(2)}) async-start(bf16[24,16,384]{2,1,0:T(8,128)(2,1)} %bitcast.25), calls=%async_computation.2 | async-start | bytes 589824 | tf_op jit(solution)/shard_map/all_to_all | solution.py:134
  63.1 117.5 %all-to-all-start.1 = ((bf16[24,16,384]{2,1,0:T(8,128)(2,1)}), bf16[24,16,384]{2,1,0:T(8,128)(2,1)S(1)}, u32[]{:S(2)}, u32[]{:S(2)}) async-start(bf16[24,16,384]{2,1,0:T(8,128)(2,1)} %copy.100), calls=%async_computation.1 | async-start | bytes 589824 | tf_op jit(solution)/shard_map/all_to_all | solution.py:123
  96.0 86.3 %copy-start.6 = (f32[256,1,128]{2,1,0:T(1,128)S(1)}, f32[256,1,128]{2,1,0:T(1,128)}, u32[]{:S(2)}) copy-start(f32[256,1,128]{2,1,0:T(1,128)} %get-tuple-element.57) | copy-start | bytes 393220
  96.0 86.3 %copy-start.7 = (f32[256,1,128]{2,1,0:T(1,128)S(1)}, f32[256,1,128]{2,1,0:T(1,128)}, u32[]{:S(2)}) copy-start(f32[256,1,128]{2,1,0:T(1,128)} %get-tuple-element.58) | copy-start | bytes 393220
  96.0 86.2 %copy-start.8 = (f32[256,1,128]{2,1,0:T(1,128)S(1)}, f32[256,1,128]{2,1,0:T(1,128)}, u32[]{:S(2)}) copy-start(f32[256,1,128]{2,1,0:T(1,128)} %get-tuple-element.59) | copy-start | bytes 393220
  96.0 86.2 %copy-start.9 = (f32[256,1,128]{2,1,0:T(1,128)S(1)}, f32[256,1,128]{2,1,0:T(1,128)}, u32[]{:S(2)}) copy-start(f32[256,1,128]{2,1,0:T(1,128)} %get-tuple-element.60) | copy-start | bytes 393220
  173.4 32.0 %collective-permute-start = (f32[16,384]{1,0:T(8,128)S(1)}, f32[16,384]{1,0:T(8,128)S(1)}, u32[]{:S(2)}, u32[]{:S(2)}) collective-permute-start(f32[16,384]{1,0:T(8,128)S(1)} %fusion), channel_id=1, source_target_pairs={{0,1},{1,2},{2,3},{3,4},{4,5},{5,6},{6,7},{7,8},{8,9},{9,10},{10,1... | collective-permute-start | bytes 73736
  175.3 30.1 %collective-permute-start.1 = (f32[16,384]{1,0:T(8,128)S(1)}, f32[16,384]{1,0:T(8,128)S(1)}, u32[]{:S(2)}, u32[]{:S(2)}) collective-permute-start(f32[16,384]{1,0:T(8,128)S(1)} %fusion), channel_id=1, source_target_pairs={{0,2},{1,3},{2,4},{3,5},{4,6},{5,7},{6,8},{7,9},{8,10},{9,11},{10,... | collective-permute-start | bytes 73736
  176.6 28.8 %collective-permute-start.2 = (f32[16,384]{1,0:T(8,128)S(1)}, f32[16,384]{1,0:T(8,128)}, u32[]{:S(2)}, u32[]{:S(2)}) collective-permute-start(f32[16,384]{1,0:T(8,128)S(1)} %fusion), channel_id=1, source_target_pairs={{0,3},{1,4},{2,5},{3,6},{4,7},{5,8},{6,9},{7,10},{8,11},{9,12},{10... | collective-permute-start | bytes 73736
  178.5 26.9 %collective-permute-start.3 = (f32[14,384]{1,0:T(8,128)S(1)}, f32[14,384]{1,0:T(8,128)}, u32[]{:S(2)}, u32[]{:S(2)}) collective-permute-start(f32[14,384]{1,0:T(8,128)S(1)} %slice.67), channel_id=1, source_target_pairs={{0,4},{1,5},{2,6},{3,7},{4,8},{5,9},{6,10},{7,11},{8,12},{9,13},{1... | collective-permute-start | bytes 64520
  188.0 4.0 %copy-start.2 = (bf16[9,9,256]{0,1,2:T(8,128)(2,1)S(1)}, bf16[9,9,256]{0,1,2:T(8,128)(2,1)}, u32[]{:S(2)}) copy-start(bf16[9,9,256]{0,1,2:T(8,128)(2,1)} %copy.106) | copy-start | bytes 124420
  188.0 4.0 %copy-start.11 = (bf16[256,1,128]{2,1,0:T(2,128)(2,1)S(1)}, bf16[256,1,128]{2,1,0:T(2,128)(2,1)}, u32[]{:S(2)}) copy-start(bf16[256,1,128]{2,1,0:T(2,128)(2,1)} %get-tuple-element.51) | copy-start | bytes 196612
  188.0 4.0 %copy-start.12 = (bf16[256,1,128]{2,1,0:T(2,128)(2,1)S(1)}, bf16[256,1,128]{2,1,0:T(2,128)(2,1)}, u32[]{:S(2)}) copy-start(bf16[256,1,128]{2,1,0:T(2,128)(2,1)} %get-tuple-element.52) | copy-start | bytes 196612
  188.0 4.0 %copy-start.13 = (bf16[256,1,128]{2,1,0:T(2,128)(2,1)S(1)}, bf16[256,1,128]{2,1,0:T(2,128)(2,1)}, u32[]{:S(2)}) copy-start(bf16[256,1,128]{2,1,0:T(2,128)(2,1)} %get-tuple-element.53) | copy-start | bytes 196612
  188.0 4.0 %copy-start.14 = (bf16[256,1,128]{2,1,0:T(2,128)(2,1)S(1)}, bf16[256,1,128]{2,1,0:T(2,128)(2,1)}, u32[]{:S(2)}) copy-start(bf16[256,1,128]{2,1,0:T(2,128)(2,1)} %get-tuple-element.54) | copy-start | bytes 196612
  195.4 9.3 %copy-start.5 = (bf16[64,9,128]{2,0,1:T(8,128)(2,1)S(1)}, bf16[64,9,128]{2,0,1:T(8,128)(2,1)}, u32[]{:S(2)}) copy-start(bf16[64,9,128]{2,0,1:T(8,128)(2,1)} %param.16) | copy-start | bytes 442372
where the time goes:
time: 257 us; the launch traced here: 255 us
  blocking collectives  124 us (48%)
  local copies, waits for them, and re-layouts  40.6 us (16%)
  starting transfers between devices  39.8 us (15%)
  other arithmetic  24.6 us (10%)
  matrix products  14.5 us (6%)
  waiting for transfers between devices  8.22 us (3%)
    unnamed x1, blocking collectives  77.4 us
    all_gather x1, blocking collectives, sum_by_parts(): whole = lax.all_gather(own, axis, axis=0, tiled=True)  46.2 us
    mul x48, local copies, waits for them, and re-layouts, add_system(): mix_row[:, None, None] * rows[None]  18 us
    all_to_all x1, starting transfers between devices, sent_to_all(): lax.all_to_all(jnp.broadcast_to(shard[None], (devices, *shard.shape)), ax...  16.9 us
    all_to_all x1, starting transfers between devices, shards(): lax.all_to_all(weight_grad.reshape(group, row_block, -1).astype(jnp.bfloa...  10 us
    scatter-add x1, other arithmetic, edge_layer(): gathered = jnp.take(feats, source, axis=0)  9.31 us
    all_to_all x1, waiting for transfers between devices, shards(): lax.all_to_all(weight_grad.reshape(group, row_block, -1).astype(jnp.bfloa...  8.21 us
    unnamed x45, local copies, waits for them, and re-layouts  8.14 us
  transfers between devices with their start and end apart: 7, of which 1 were waited for; matrix products, arithmetic and copies ran while one was open for 58% of the time, Pallas kernels for 0%

commit v1 on v0

v1 whole, which is shorter than its diff:
```python
import math

import jax
import jax.numpy as jnp
from jax import lax
from jax.experimental import pallas as pl
from jax.experimental.pallas import tpu as pltpu
from jax.sharding import PartitionSpec as P

BF16 = jnp.bfloat16
F32 = jnp.float32
CHUNK = 16
PARTS = 3


def iota(shape, dim):
    return lax.broadcasted_iota(jnp.int32, shape, dim)


def dot(a, b, contract):
    return lax.dot_general(a, b, ((contract[:1], contract[1:]), ((), ())), preferred_element_type=F32)


def one_hot(index_row, count):
    return iota((count, index_row.shape[1]), 0) == index_row


def split(value):
    parts = []
    for _ in range(PARTS):
        part = value.astype(BF16)
        parts.append(part)
        value = value - part.astype(F32)
    return parts


def mixture_row(types_ref, dataset_ref, type_table_ref, dataset_table_ref, router_ref):
    table = type_table_ref[...]
    atoms = types_ref.shape[1]
    counts = jnp.sum(one_hot(types_ref[...], table.shape[0]).astype(F32), axis=1, keepdims=True)
    embed = jnp.sum(counts * table, axis=0, keepdims=True) / atoms
    data_table = dataset_table_ref[...]
    pick = (iota((data_table.shape[0], 1), 0) == dataset_ref[...]).astype(F32)
    embed = embed + jnp.sum(pick * data_table, axis=0, keepdims=True)
    logits = jnp.sum(router_ref[...] * embed, axis=1, keepdims=True)
    soft = jnp.maximum(logits, 0.0) + jnp.log1p(jnp.exp(-jnp.abs(logits)))
    mixture = soft / jnp.sum(soft, axis=0, keepdims=True)
    shape = (mixture.shape[0], 128)
    return jnp.sum(jnp.where(iota(shape, 0) == iota(shape, 1), mixture, 0.0), axis=0, keepdims=True)


def spread(feats_ref, cot_ref, source_ref, target_ref, valid_ref, gathered_ref, back_ref, scale):
    atoms = feats_ref.shape[1]
    source = one_hot(source_ref[...], atoms).astype(BF16)
    incidence = (one_hot(target_ref[...], atoms) & (valid_ref[...] > 0)).astype(BF16)
    for j in range(feats_ref.shape[0]):
        gathered_ref[j] = dot(feats_ref[j], source, (0, 0))
        back_ref[j] = dot(cot_ref[j], incidence, (0, 0)) * scale
    return source, incidence


def rotate(frames_ref, rows, values, transposed=False):
    count = len(values)
    out = []
    for i in rows:
        total = None
        for j in range(count):
            row = frames_ref[j, i : i + 1, :] if transposed else frames_ref[i, j : j + 1, :]
            term = row * values[j]
            total = term if total is None else total + term
        out.append(total)
    return out


def first_kernel(
    group,
    zero_rows,
    scale,
    feats_ref,
    cot_ref,
    frames_ref,
    radial_ref,
    source_ref,
    target_ref,
    valid_ref,
    types_ref,
    dataset_ref,
    type_table_ref,
    dataset_table_ref,
    router_ref,
    out_ref,
    frames32_ref,
    gathered_ref,
    back_ref,
    gate_ref,
    band_ref,
    mixed_ref,
):
    comps, _, channels = feats_ref.shape
    frames32_ref[...] = frames_ref[...].astype(F32)
    gate_ref[...] = radial_ref[...].astype(F32).T
    spread(feats_ref, cot_ref, source_ref, target_ref, valid_ref, gathered_ref, back_ref, scale)

    def chunk(step, carry):
        at = pl.ds(pl.multiple_of(step * CHUNK, CHUNK), CHUNK)
        values = [gathered_ref[j, at, :] for j in range(comps)]
        for n, total in enumerate(rotate(frames32_ref, zero_rows, values)):
            band_ref[n, at, :] = total.astype(BF16)
        values = [back_ref[j, at, :] for j in range(comps)]
        gate = gate_ref[at, :]
        for n, total in enumerate(rotate(frames32_ref, zero_rows, values)):
            mixed_ref[n, at, :] = (total.astype(BF16).astype(F32) * gate).astype(BF16)
        return carry

    lax.fori_loop(0, channels // CHUNK, chunk, 0)
    width = len(zero_rows) * channels
    edges = band_ref.shape[2]
    band = band_ref[...].reshape(width, edges)
    block = width // group
    for n in range(len(zero_rows)):
        grad = dot(band, mixed_ref[n], (1, 1)).astype(BF16)
        out_ref[:, n * block : (n + 1) * block, :] = grad.reshape(group, block, channels)
    row = mixture_row(types_ref, dataset_ref, type_table_ref, dataset_table_ref, router_ref)
    spare = out_ref.shape[1] - len(zero_rows) * block
    tail = jnp.concatenate(
        [part.astype(F32) for part in split(row)] + [jnp.zeros((spare - PARTS, channels), F32)], axis=0
    ).astype(BF16)
    out_ref[:, len(zero_rows) * block :, :] = jnp.broadcast_to(tail[None], (group, spare, channels))


def second_kernel(experts_count, recv_ref, experts_ref, shares_ref, sums_ref):
    group, lines, channels = recv_ref.shape
    total_rows, width = experts_ref.shape
    block = total_rows // experts_count
    pieces = width // channels
    rows = group * block
    tail = recv_ref[:, pieces * block :, :].astype(F32)
    spread_systems = (iota((rows, group), 0) // block == iota((rows, group), 1)).astype(BF16)
    spread_experts = (iota((channels, total_rows), 1) // block == iota((channels, total_rows), 0)).astype(BF16)
    collect_experts = (iota((total_rows, channels), 0) // block == iota((total_rows, channels), 1)).astype(BF16)
    collect_systems = (iota((group, rows), 1) // block == iota((group, rows), 0)).astype(BF16)
    same = iota((rows, total_rows), 0) % block == iota((rows, total_rows), 1) % block
    same_back = iota((total_rows, rows), 0) % block == iota((total_rows, rows), 1) % block
    experts = experts_ref[...]
    shares = None
    back = []
    for p in range(PARTS):
        part = tail[:, p, :].astype(BF16)
        wide = dot(dot(spread_systems, part, (1, 0)).astype(BF16), spread_experts, (1, 0))
        wide = jnp.where(same, wide, 0.0).astype(BF16)
        term = dot(wide, experts, (1, 0))
        shares = term if shares is None else shares + term
        if p < 2:
            wide = dot(dot(collect_experts, part, (1, 1)).astype(BF16), collect_systems, (1, 0))
            back.append(jnp.where(same_back, wide, 0.0).astype(BF16))
    shares_ref[...] = shares.astype(BF16).reshape(shares_ref.shape)
    for n in range(pieces):
        grads = recv_ref[:, n * block : (n + 1) * block, :].reshape(rows, channels)
        total = dot(back[0], grads, (1, 0)) + dot(back[1], grads, (1, 0))
        sums_ref[:experts_count, :, n * channels : (n + 1) * channels] = total.astype(BF16).reshape(
            experts_count, block, channels
        )
    spare = sums_ref.shape[0] - experts_count
    if spare:
        sums_ref[experts_count:] = jnp.zeros((spare, *sums_ref.shape[1:]), BF16)


def sum_kernel(parts_ref, out_ref):
    total = jnp.sum(parts_ref[...].astype(F32), axis=0)
    out_ref[...] = jnp.broadcast_to(total.astype(BF16)[None], out_ref.shape)


def layer_kernel(
    zero_rows,
    scale,
    feats_ref,
    cot_ref,
    frames_ref,
    radial_ref,
    source_ref,
    target_ref,
    valid_ref,
    merged_ref,
    updated_ref,
    grad_ref,
    frames32_ref,
    gathered_ref,
    back_ref,
    gate_ref,
    rotated_ref,
    turned_ref,
    mixed_ref,
    band_grad_ref,
):
    comps, _, channels = feats_ref.shape
    edges = radial_ref.shape[0]
    width = merged_ref.shape[0]
    frames32_ref[...] = frames_ref[...].astype(F32)
    gate_ref[...] = radial_ref[...].astype(F32).T
    source, incidence = spread(
        feats_ref, cot_ref, source_ref, target_ref, valid_ref, gathered_ref, back_ref, scale
    )

    def forth(step, carry):
        at = pl.ds(pl.multiple_of(step * CHUNK, CHUNK), CHUNK)
        values = [gathered_ref[j, at, :] for j in range(comps)]
        for n, total in enumerate(rotate(frames32_ref, range(comps), values)):
            rotated_ref[n, at, :] = total.astype(BF16)
        values = [back_ref[j, at, :] for j in range(comps)]
        gate = gate_ref[at, :]
        for n, total in enumerate(rotate(frames32_ref, range(comps), values)):
            turned_ref[n, at, :] = (total.astype(BF16).astype(F32) * gate).astype(BF16)
        return carry

    lax.fori_loop(0, channels // CHUNK, forth, 0)
    merged = merged_ref[...]
    band = jnp.concatenate([rotated_ref[row] for row in zero_rows], axis=0)
    mixed_ref[...] = dot(merged, band, (0, 0)).reshape(len(zero_rows), channels, edges)
    turned = jnp.concatenate([turned_ref[row] for row in zero_rows], axis=0)
    band_grad_ref[...] = dot(merged, turned, (1, 0)).astype(BF16).reshape(len(zero_rows), channels, edges)

    def back(step, carry):
        at = pl.ds(pl.multiple_of(step * CHUNK, CHUNK), CHUNK)
        gate = gate_ref[at, :]
        values = []
        for row in range(comps):
            if row in zero_rows:
                value = mixed_ref[zero_rows.index(row), at, :]
            else:
                value = rotated_ref[row, at, :].astype(F32)
            values.append((value * gate).astype(BF16).astype(F32))
        for n, total in enumerate(rotate(frames32_ref, range(comps), values, True)):
            gathered_ref[n, at, :] = total
        values = []
        for row in range(comps):
            if row in zero_rows:
                values.append(band_grad_ref[zero_rows.index(row), at, :].astype(F32))
            else:
                values.append(turned_ref[row, at, :].astype(F32))
        for n, total in enumerate(rotate(frames32_ref, range(comps), values, True)):
            back_ref[n, at, :] = total
        return carry

    lax.fori_loop(0, channels // CHUNK, back, 0)
    for j in range(comps):
        summed = dot(incidence, gathered_ref[j].astype(BF16), (1, 1))
        updated_ref[j] = (feats_ref[j].astype(F32) + summed * scale).astype(BF16)
        summed = dot(source, back_ref[j].astype(BF16), (1, 1))
        grad_ref[j] = cot_ref[j].astype(F32) + summed.astype(BF16).astype(F32)


def call(kernel, outs, scratch, flops, *args):
    size = sum(math.prod(a.shape) * a.dtype.itemsize for a in (*args, *outs))
    return pl.pallas_call(
        kernel,
        out_shape=outs,
        in_specs=[pl.BlockSpec(memory_space=pltpu.VMEM)] * len(args),
        out_specs=[pl.BlockSpec(memory_space=pltpu.VMEM)] * len(outs),
        scratch_shapes=scratch,
        cost_estimate=pl.CostEstimate(flops=flops, bytes_accessed=size, transcendentals=0),
        compiler_params=pltpu.CompilerParams(vmem_limit_bytes=32 * 1024 * 1024),
    )(*args)


def shards(
    atom_feats,
    cotangent,
    frames,
    radial,
    edge_source,
    edge_target,
    edge_valid,
    atom_types,
    dataset,
    type_table,
    dataset_table,
    router_weight,
    experts,
):
    group = lax.axis_size("shard")
    replicas = lax.axis_size("replica")
    expert_count, block, width = experts.shape
    atoms, comps, channels = atom_feats.shape
    edges = radial.shape[0]
    degrees = math.isqrt(comps)
    zero_rows = [degree * degree + degree for degree in range(degrees)]
    scale = atoms / edges
    feats = atom_feats.transpose(1, 0, 2)
    cot = cotangent.transpose(1, 0, 2)
    edge_args = (
        feats,
        cot,
        frames,
        radial,
        edge_source[None],
        edge_target[None],
        edge_valid[None],
    )
    planes = (comps, channels, edges)
    bands = (degrees, channels, edges)
    common = [
        pltpu.VMEM(frames.shape, F32),
        pltpu.VMEM(planes, F32),
        pltpu.VMEM(planes, F32),
        pltpu.VMEM((channels, edges), F32),
    ]

    def first(*refs):
        first_kernel(group, zero_rows, scale, *refs)

    lines = degrees * block + 8
    (sent,) = call(
        first,
        [jax.ShapeDtypeStruct((group, lines, channels), BF16)],
        common + [pltpu.VMEM(bands, BF16), pltpu.VMEM(bands, BF16)],
        10**9,
        *edge_args,
        atom_types[None],
        dataset[None],
        type_table,
        dataset_table,
        router_weight.T,
    )
    received = lax.all_to_all(sent, "shard", 0, 0, tiled=True)

    def second(*refs):
        second_kernel(expert_count, *refs)

    shares, sums = call(
        second,
        [
            jax.ShapeDtypeStruct((group, block, width), BF16),
            jax.ShapeDtypeStruct((replicas, block, width), BF16),
        ],
        [],
        10**9,
        received,
        experts.reshape(expert_count * block, width),
    )
    merged = lax.all_to_all(shares, "shard", 0, 0, tiled=True).reshape(group * block, width)
    parts = lax.all_to_all(sums, "replica", 0, 0, tiled=True)
    (own,) = call(sum_kernel, [jax.ShapeDtypeStruct(parts.shape, BF16)], [], 10**7, parts)
    whole = lax.all_to_all(own, "replica", 0, 0, tiled=True)
    expert_grad = whole[:expert_count].astype(F32)

    def layer(*refs):
        layer_kernel(zero_rows, scale, *refs)

    updated, feats_grad = call(
        layer,
        [jax.ShapeDtypeStruct(feats.shape, BF16), jax.ShapeDtypeStruct(feats.shape, F32)],
        common
        + [
            pltpu.VMEM(planes, BF16),
            pltpu.VMEM(planes, BF16),
            pltpu.VMEM(bands, F32),
            pltpu.VMEM(bands, BF16),
        ],
        5 * 10**9,
        *edge_args,
        merged,
    )
    return (updated.transpose(1, 0, 2), feats_grad.transpose(1, 0, 2), expert_grad)


def solution(mesh):
    both = ("shard", "replica")
    in_specs = (
        P(both, None, None),
        P(both, None, None),
        P(None, None, both),
        P(both, None),
        P(both),
        P(both),
        P(both),
        P(both),
        P(both),
        P(),
        P(),
        P(),
        P(None, "shard", None),
    )
    out_specs = (P(both, None, None), P(both, None, None), P(None, "shard", None))
    return jax.shard_map(shards, mesh=mesh, in_specs=in_specs, out_specs=out_specs, check_vma=False)
```

time: 257 us -> 117 us (0.46)
  blocking collectives: 124 us -> 60.1 us
  local copies, waits for them, and re-layouts: 40.6 us -> 8.37 us
  starting transfers between devices: 39.8 us -> 11.3 us
  other arithmetic: 24.6 us -> 0.89 us
  waiting for transfers between devices: 8.22 us -> 23.8 us
  matrix products: 14.5 us -> 0 us
  Pallas kernels: 0 us -> 10.1 us
    unnamed x1 -> x0, blocking collectives: 77.4 us -> none
    all_to_all x0 -> x2, blocking collectives: none -> 60.1 us  [the longest x1 33 us: shards(): received = lax.all_to_all(sent, 'shard', 0, 0, tiled=True)]
    all_gather x1 -> x0, blocking collectives: 46.2 us -> none  [sum_by_parts(): whole = lax.all_gather(own, axis, axis=0, tiled=True)]
    all_to_all x3 -> x2, starting transfers between devices: 32.6 us -> 11.3 us  [the longest x1 6.6 us: shards(): whole = lax.all_to_all(own, 'replica', 0, 0, tiled=True)]
    mul x48 -> x0, local copies, waits for them, and re-layouts: 18 us -> none  [add_system(): mix_row[:, None, None] * rows[None]]
    all_to_all x3 -> x2, waiting for transfers between devices: 8.21 us -> 23.8 us  [the longest x1 14.3 us: shards(): lax.all_to_all(shares, 'shard', 0, 0, tiled=True)]
    dot_general x13 -> x0, matrix products: 14.5 us -> none  [the longest x2 4.02 us: edge_layer(): jnp.einsum('jie,ejc->eic', frames.astype(jnp.float32), message.astype(jnp...]
    pallas_call x0 -> x4, Pallas kernels: none -> 10.1 us  [call(): pl.pallas_call(kernel, out_shape=outs, in_specs=[pl.BlockSpec(memory_spac...]
  transfers between devices with their start and end apart: 7 -> 2, of which waited for: 1 -> 2; matrix products, arithmetic and copies ran while one was open for 58% -> 0% of each run, Pallas kernels for 0% -> 5%
where the time goes in v1:
time: 117 us; the launch traced here: 116 us
  blocking collectives  60.1 us (51%)
  waiting for transfers between devices  23.8 us (20%)
  starting transfers between devices  11.3 us (10%)
  Pallas kernels  10.1 us (9%)
  local copies, waits for them, and re-layouts  8.37 us (7%)
  between operations  1.4 us (1%)
    all_to_all x1, blocking collectives, shards(): received = lax.all_to_all(sent, 'shard', 0, 0, tiled=True)  33 us
    all_to_all x1, blocking collectives, shards(): parts = lax.all_to_all(sums, 'replica', 0, 0, tiled=True)  27.1 us
    all_to_all x1, waiting for transfers between devices, shards(): lax.all_to_all(shares, 'shard', 0, 0, tiled=True)  14.3 us
    pallas_call x4, Pallas kernels, call(): pl.pallas_call(kernel, out_shape=outs, in_specs=[pl.BlockSpec(memory_spac...  10.1 us
    all_to_all x1, waiting for transfers between devices, shards(): whole = lax.all_to_all(own, 'replica', 0, 0, tiled=True)  9.54 us
    unnamed x36, local copies, waits for them, and re-layouts  8.37 us
    all_to_all x1, starting transfers between devices, shards(): whole = lax.all_to_all(own, 'replica', 0, 0, tiled=True)  6.6 us
    all_to_all x1, starting transfers between devices, shards(): lax.all_to_all(shares, 'shard', 0, 0, tiled=True)  4.68 us
  transfers between devices with their start and end apart: 2, of which 2 were waited for; matrix products, arithmetic and copies ran while one was open for 0% of the time, Pallas kernels for 5%

profile of v1, /device:TPU:1, one launch (start us, length us, event | category | flops | bytes accessed | tf_op | source)
XLA Modules:
  0.0 116.0 jit_solution(14094567744992554463)
XLA Ops:
  0.6 0.0 copy-start.10
  1.3 0.0 copy-start.12
  1.3 0.0 copy-done.10
  1.4 0.6 copy-done.12
  2.0 0.9 copy-done.1
  2.9 0.9 copy-done.3
  3.8 0.9 copy-done.5
  4.7 0.8 copy-done.7
  5.5 0.8 copy-done.9
  6.3 0.7 copy-done.11
  7.0 0.7 copy-done.13
  7.7 0.7 copy-done.15
  8.4 0.7 copy-done.17
  9.0 1.4 %shard_map.148 = bf16[24,56,128]{2,1,0:T(8,128)(2,1)S(1)} custom-call(bf16[9,64,128]{2,1,0:T(8,128)(2,1)S(1)} %bitcast.15, bf16[9,64,128]{2,1,0:T(8,128)(2,1)S(1)} %bitcast.17, bf16[9,9,256]{2,1,0:T(8,128)(2,1)S(1)} %copy-done.5, bf16[256,128]{1,0:T(8,128)(2,1)S(1)} %copy-done.7, s32[1,256]{1,0:T(1,128)S(1)} %bitcast.20, s32[1,256]{1,0:T(1,128)S(1)} %bitcast.22, ...), custom_call_target="tpu_custom_call" | custom-call | flops 1000000000 | bytes 817412 | tf_op jit(solution)/shard_map/pallas_call | solution.py:254
  10.5 0.0 copy-start
  10.5 33.0 %all_to_all.20.refs_0_ = bf16[24,56,128]{2,1,0:T(8,128)(2,1)S(1)} all-to-all(bf16[24,56,128]{2,1,0:T(8,128)(2,1)S(1)} %shard_map.148), channel_id=1, replica_groups=mesh['shard'=24,'replica'=32] {'shard'}, dimensions={0} | all-to-all | bytes 688128 | tf_op jit(solution)/shard_map/all_to_all | solution.py:324
  43.5 0.0 copy-done
  43.5 2.7 %shard_map.149 = (bf16[24,16,384]{2,1,0:T(8,128)(2,1)}, bf16[32,16,384]{2,1,0:T(8,128)(2,1)S(1)}) custom-call(bf16[24,56,128]{2,1,0:T(8,128)(2,1)S(1)} %all_to_all.20.refs_0_, bf16[448,384]{1,0:T(8,128)(2,1)S(1)} %bitcast.14), custom_call_target="tpu_custom_call" | custom-call | flops 1000000000 | bytes 1376256 | tf_op jit(solution)/shard_map/pallas_call | solution.py:254
  46.2 27.1 %all_to_all.21.parts_ref = bf16[32,16,384]{2,1,0:T(8,128)(2,1)S(1)} all-to-all(bf16[32,16,384]{2,1,0:T(8,128)(2,1)S(1)} %get-tuple-element.10), channel_id=1, replica_groups=mesh['shard'=24,'replica'=32] {'replica'}, dimensions={0} | all-to-all | bytes 786432 | tf_op jit(solution)/shard_map/all_to_all | solution.py:341
  73.3 4.7 %all-to-all-start.1 = ((bf16[24,16,384]{2,1,0:T(8,128)(2,1)}), bf16[24,16,384]{2,1,0:T(8,128)(2,1)S(1)}, u32[]{:S(2)}, u32[]{:S(2)}) async-start(bf16[24,16,384]{2,1,0:T(8,128)(2,1)} %get-tuple-element.7), calls=%async_computation.1 | async-start | bytes 589824 | tf_op jit(solution)/shard_map/all_to_all | solution.py:340
  78.0 0.8 shard_map.151
  78.8 14.3 %all-to-all-done.1 = bf16[24,16,384]{2,1,0:T(8,128)(2,1)S(1)} async-done(((bf16[24,16,384]{2,1,0:T(8,128)(2,1)}), bf16[24,16,384]{2,1,0:T(8,128)(2,1)S(1)}, u32[]{:S(2)}, u32[]{:S(2)}) %all-to-all-start.1) | async-done | bytes 294944 | tf_op jit(solution)/shard_map/all_to_all | solution.py:340
  93.1 6.6 %all-to-all-start.3 = ((bf16[32,16,384]{2,1,0:T(8,128)(2,1)}), bf16[32,16,384]{2,1,0:T(8,128)(2,1)S(1)}, u32[]{:S(2)}, u32[]{:S(2)}) async-start(bf16[32,16,384]{2,1,0:T(8,128)(2,1)} %shard_map.151), calls=%async_computation.3 | async-start | bytes 786432 | tf_op jit(solution)/shard_map/all_to_all | solution.py:343
  99.7 0.0 copy-start.14
  99.7 0.0 copy-done.2
  99.7 0.0 copy-done.4
  99.7 0.0 copy-done.6
  99.7 0.0 copy-done.8
  99.8 0.6 copy-done.14
  100.4 5.2 %shard_map.150 = (bf16[9,64,128]{2,1,0:T(8,128)(2,1)}, f32[9,64,128]{2,1,0:T(8,128)}) custom-call(bf16[9,64,128]{2,1,0:T(8,128)(2,1)S(1)} %bitcast.16, bf16[9,64,128]{2,1,0:T(8,128)(2,1)S(1)} %bitcast.18, bf16[9,9,256]{2,1,0:T(8,128)(2,1)S(1)} %copy-done.6, bf16[256,128]{1,0:T(8,128)(2,1)S(1)} %copy-done.8, s32[1,256]{1,0:T(1,128)S(1)} %bitcast.21, ...), custom_call_target="tpu_custom_call" | custom-call | flops 5000000000 | bytes 1142272 | tf_op jit(solution)/shard_map/pallas_call | solution.py:254
  105.5 9.5 %all-to-all-done.3 = bf16[32,16,384]{2,1,0:T(8,128)(2,1)S(1)} async-done(((bf16[32,16,384]{2,1,0:T(8,128)(2,1)}), bf16[32,16,384]{2,1,0:T(8,128)(2,1)S(1)}, u32[]{:S(2)}, u32[]{:S(2)}) %all-to-all-start.3) | async-done | bytes 393248 | tf_op jit(solution)/shard_map/all_to_all | solution.py:343
  115.1 0.9 slice_convert_fusion
  (15 shorter events, 0.0 us)
Async XLA Ops:
  0.6 0.7 copy-start.10
  1.3 0.7 copy-start.12
  2.0 0.9 copy-start.1
  2.9 0.9 copy-start.3
  3.8 0.9 copy-start.5
  4.7 0.8 copy-start.7
  5.5 0.8 copy-start.9
  6.3 0.7 copy-start.11
  7.0 0.7 copy-start.13
  7.7 0.7 copy-start.15
  8.4 0.7 copy-start.17
  10.5 33.0 %copy-start = (bf16[28,16,384]{2,1,0:T(8,128)(2,1)S(1)}, bf16[28,16,384]{2,1,0:T(8,128)(2,1)}, u32[]{:S(2)}) copy-start(bf16[28,16,384]{2,1,0:T(8,128)(2,1)} %param.25) | copy-start | bytes 1032196
  73.3 19.8 %all-to-all-start.1 = ((bf16[24,16,384]{2,1,0:T(8,128)(2,1)}), bf16[24,16,384]{2,1,0:T(8,128)(2,1)S(1)}, u32[]{:S(2)}, u32[]{:S(2)}) async-start(bf16[24,16,384]{2,1,0:T(8,128)(2,1)} %get-tuple-element.7), calls=%async_computation.1 | async-start | bytes 589824 | tf_op jit(solution)/shard_map/all_to_all | solution.py:340
  78.8 20.9 %copy-start.2 = (bf16[64,9,128]{2,0,1:T(8,128)(2,1)S(1)}, bf16[64,9,128]{2,0,1:T(8,128)(2,1)}, u32[]{:S(2)}) copy-start(bf16[64,9,128]{2,0,1:T(8,128)(2,1)} %param.13) | copy-start | bytes 442372
  78.8 20.9 %copy-start.4 = (bf16[64,9,128]{2,0,1:T(8,128)(2,1)S(1)}, bf16[64,9,128]{2,0,1:T(8,128)(2,1)}, u32[]{:S(2)}) copy-start(bf16[64,9,128]{2,0,1:T(8,128)(2,1)} %param.14) | copy-start | bytes 442372
  78.8 20.9 %copy-start.6 = (bf16[9,9,256]{2,1,0:T(8,128)(2,1)S(1)}, bf16[9,9,256]{2,1,0:T(8,128)(2,1)}, u32[]{:S(2)}) copy-start(bf16[9,9,256]{2,1,0:T(8,128)(2,1)} %refs_2_.3) | copy-start | bytes 124420
  78.8 20.9 %copy-start.8 = (bf16[256,128]{1,0:T(8,128)(2,1)S(1)}, bf16[256,128]{1,0:T(8,128)(2,1)}, u32[]{:S(2)}) copy-start(bf16[256,128]{1,0:T(8,128)(2,1)} %refs_3_.3) | copy-start | bytes 196612
  93.1 6.7 %copy-start.16 = (s32[256]{0:T(256)S(1)}, s32[256]{0:T(256)}, u32[]{:S(2)}) copy-start(s32[256]{0:T(256)} %param.19) | copy-start | bytes 3076
  93.1 22.0 %all-to-all-start.3 = ((bf16[32,16,384]{2,1,0:T(8,128)(2,1)}), bf16[32,16,384]{2,1,0:T(8,128)(2,1)S(1)}, u32[]{:S(2)}, u32[]{:S(2)}) async-start(bf16[32,16,384]{2,1,0:T(8,128)(2,1)} %shard_map.151), calls=%async_computation.3 | async-start | bytes 786432 | tf_op jit(solution)/shard_map/all_to_all | solution.py:343
  99.7 0.7 copy-start.14

commit v2 on v1

--- a/solution.py
+++ b/solution.py
@@ -5,12 +5,15 @@
 from jax import lax
 from jax.experimental import pallas as pl
 from jax.experimental.pallas import tpu as pltpu
+from jax.sharding import Mesh
 from jax.sharding import PartitionSpec as P
+
 
 BF16 = jnp.bfloat16
 F32 = jnp.float32
 CHUNK = 16
 PARTS = 3
+REPLICA_SIZES = (4, 4, 2)
 
 
 def iota(shape, dim):
@@ -72,30 +75,25 @@
     return out
 
 
-def first_kernel(
-    group,
-    zero_rows,
-    scale,
-    feats_ref,
-    cot_ref,
-    frames_ref,
-    radial_ref,
-    source_ref,
-    target_ref,
-    valid_ref,
-    types_ref,
-    dataset_ref,
-    type_table_ref,
-    dataset_table_ref,
-    router_ref,
-    out_ref,
-    frames32_ref,
-    gathered_ref,
-    back_ref,
-    gate_ref,
-    band_ref,
-    mixed_ref,
-):
+def first_kernel(group, zero_rows, scale, *refs):
+    count = 12
+    sources, (out_ref,), refs = refs[:count], refs[count : count + 1], refs[count + 1 :]
+    inputs, refs = refs[:count], refs[count:]
+    frames32_ref, gathered_ref, back_ref, gate_ref, band_ref, mixed_ref, sems = refs
+    copies = [
+        pltpu.make_async_copy(source, target, sems.at[n])
+        for n, (source, target) in enumerate(zip(sources, inputs))
+    ]
+    for copy in copies:
+        copy.start()
+    router_args, edge_args = inputs[:5], inputs[5:]
+    for copy in copies[:5]:
+        copy.wait()
+    row = mixture_row(*router_args)
+    group_lines = out_ref.shape[1]
+    source_ref, target_ref, valid_ref, feats_ref, cot_ref, frames_ref, radial_ref = edge_args
+    for copy in copies[5:]:
+        copy.wait()
     comps, _, channels = feats_ref.shape
     frames32_ref[...] = frames_ref[...].astype(F32)
     gate_ref[...] = radial_ref[...].astype(F32).T
@@ -120,54 +118,69 @@
     for n in range(len(zero_rows)):
         grad = dot(band, mixed_ref[n], (1, 1)).astype(BF16)
         out_ref[:, n * block : (n + 1) * block, :] = grad.reshape(group, block, channels)
-    row = mixture_row(types_ref, dataset_ref, type_table_ref, dataset_table_ref, router_ref)
-    spare = out_ref.shape[1] - len(zero_rows) * block
+    spare = group_lines - len(zero_rows) * block
     tail = jnp.concatenate(
         [part.astype(F32) for part in split(row)] + [jnp.zeros((spare - PARTS, channels), F32)], axis=0
     ).astype(BF16)
     out_ref[:, len(zero_rows) * block :, :] = jnp.broadcast_to(tail[None], (group, spare, channels))
 
 
-def second_kernel(experts_count, recv_ref, experts_ref, shares_ref, sums_ref):
-    group, lines, channels = recv_ref.shape
-    total_rows, width = experts_ref.shape
-    block = total_rows // experts_count
-    pieces = width // channels
+def tail_rows(recv_ref, block):
+    channels = recv_ref.shape[2]
+    lines = recv_ref.shape[1] - recv_ref.shape[1] % block
+    return recv_ref[:, lines:, :].astype(F32), lines // block, channels
+
+
+def sums_kernel(expert_count, block, order, recv_ref, sums_ref):
+    tail, pieces, channels = tail_rows(recv_ref, block)
+    group = recv_ref.shape[0]
+    rows, total_rows = group * block, expert_count * block
+    collect_experts = (iota((total_rows, channels), 0) // block == iota((total_rows, channels), 1)).astype(BF16)
+    collect_systems = (iota((group, rows), 1) // block == iota((group, rows), 0)).astype(BF16)
+    same = iota((total_rows, rows), 0) % block == iota((total_rows, rows), 1) % block
+    weights = []
+    for p in range(2):
+        part = tail[:, p, :].astype(BF16)
+        wide = dot(dot(collect_experts, part, (1, 1)).astype(BF16), collect_systems, (1, 0))
+        weights.append(jnp.where(same, wide, 0.0).astype(BF16))
+    for n in range(pieces):
+        grads = recv_ref[:, n * block : (n + 1) * block, :].reshape(rows, channels)
+        total = (dot(weights[0], grads, (1, 0)) + dot(weights[1], grads, (1, 0))).astype(BF16)
+        piece = sums_ref.shape[1]
+        for member, at in enumerate(order):
+            rows_here = max(0, min(piece, total_rows - at * piece))
+            lanes = slice(n * channels, (n + 1) * channels)
+            if rows_here:
+                sums_ref[member, :rows_here, lanes] = total[at * piece : at * piece + rows_here]
+            if rows_here < piece:
+                sums_ref[member, rows_here:, lanes] = jnp.zeros((piece - rows_here, channels), BF16)
+
+
+def shares_kernel(block, recv_ref, experts_ref, shares_ref):
+    tail, _, channels = tail_rows(recv_ref, block)
+    group = recv_ref.shape[0]
+    total_rows, _ = experts_ref.shape
     rows = group * block
-    tail = recv_ref[:, pieces * block :, :].astype(F32)
     spread_systems = (iota((rows, group), 0) // block == iota((rows, group), 1)).astype(BF16)
     spread_experts = (iota((channels, total_rows), 1) // block == iota((channels, total_rows), 0)).astype(BF16)
-    collect_experts = (iota((total_rows, channels), 0) // block == iota((total_rows, channels), 1)).astype(BF16)
-    collect_systems = (iota((group, rows), 1) // block == iota((group, rows), 0)).astype(BF16)
     same = iota((rows, total_rows), 0) % block == iota((rows, total_rows), 1) % block
-    same_back = iota((total_rows, rows), 0) % block == iota((total_rows, rows), 1) % block
     experts = experts_ref[...]
     shares = None
-    back = []
     for p in range(PARTS):
         part = tail[:, p, :].astype(BF16)
         wide = dot(dot(spread_systems, part, (1, 0)).astype(BF16), spread_experts, (1, 0))
-        wide = jnp.where(same, wide, 0.0).astype(BF16)
-        term = dot(wide, experts, (1, 0))
+        term = dot(jnp.where(same, wide, 0.0).astype(BF16), experts, (1, 0))
         shares = term if shares is None else shares + term
-        if p < 2:
-            wide = dot(dot(collect_experts, part, (1, 1)).astype(BF16), collect_systems, (1, 0))
-            back.append(jnp.where(same_back, wide, 0.0).astype(BF16))
-    shares_ref[...] = shares.astype(BF16).reshape(shares_ref.shape)
-    for n in range(pieces):
-        grads = recv_ref[:, n * block : (n + 1) * block, :].reshape(rows, channels)
-        total = dot(back[0], grads, (1, 0)) + dot(back[1], grads, (1, 0))
-        sums_ref[:experts_count, :, n * channels : (n + 1) * channels] = total.astype(BF16).reshape(
-            experts_count, block, channels
-        )
-    spare = sums_ref.shape[0] - experts_count
-    if spare:
-        sums_ref[experts_count:] = jnp.zeros((spare, *sums_ref.shape[1:]), BF16)
+    shares_ref[...] = shares.astype(BF16)
 
 
 def sum_kernel(parts_ref, out_ref):
-    total = jnp.sum(parts_ref[...].astype(F32), axis=0)
-    out_ref[...] = jnp.broadcast_to(total.astype(BF16)[None], out_ref.shape)
+    out_ref[...] = jnp.sum(parts_ref[...].astype(F32), axis=0).astype(BF16)
+
+
+def pair_kernel(own_ref, other_ref, out_ref):
+    total = (own_ref[...].astype(F32) + other_ref[...].astype(F32)).astype(BF16)
+    out_ref[...] = jnp.broadcast_to(total, out_ref.shape)
 
 
 def layer_kernel(
@@ -194,7 +207,6 @@
 ):
     comps, _, channels = feats_ref.shape
     edges = radial_ref.shape[0]
-    width = merged_ref.shape[0]
     frames32_ref[...] = frames_ref[...].astype(F32)
     gate_ref[...] = radial_ref[...].astype(F32).T
     source, incidence = spread(
@@ -249,17 +261,26 @@
         grad_ref[j] = cot_ref[j].astype(F32) + summed.astype(BF16).astype(F32)
 
 
-def call(kernel, outs, scratch, flops, *args):
+def call(kernel, outs, scratch, flops, *args, space=pltpu.VMEM, limit=32 * 1024):
     size = sum(math.prod(a.shape) * a.dtype.itemsize for a in (*args, *outs))
     return pl.pallas_call(
         kernel,
         out_shape=outs,
-        in_specs=[pl.BlockSpec(memory_space=pltpu.VMEM)] * len(args),
+        in_specs=[pl.BlockSpec(memory_space=space)] * len(args),
         out_specs=[pl.BlockSpec(memory_space=pltpu.VMEM)] * len(outs),
         scratch_shapes=scratch,
         cost_estimate=pl.CostEstimate(flops=flops, bytes_accessed=size, transcendentals=0),
-        compiler_params=pltpu.CompilerParams(vmem_limit_bytes=32 * 1024 * 1024),
+        compiler_params=pltpu.CompilerParams(vmem_limit_bytes=limit * 1024),
     )(*args)
+
+
+def summed_over_pairs(rows, axis, copies):
+    size = lax.axis_size(axis)
+    for n, turn in enumerate((1, size - 1)):
+        other = lax.ppermute(rows, axis, [(i, i ^ turn) for i in range(size)])
+        shape = (copies, *rows.shape) if n else rows.shape
+        (rows,) = call(pair_kernel, [jax.ShapeDtypeStruct(shape, BF16)], [], 10**6, rows, other)
+    return rows
 
 
 def shards(
@@ -278,7 +299,6 @@
     experts,
 ):
     group = lax.axis_size("shard")
-    replicas = lax.axis_size("replica")
     expert_count, block, width = experts.shape
     atoms, comps, channels = atom_feats.shape
     edges = radial.shape[0]
@@ -287,15 +307,7 @@
     scale = atoms / edges
     feats = atom_feats.transpose(1, 0, 2)
     cot = cotangent.transpose(1, 0, 2)
-    edge_args = (
-        feats,
-        cot,
-        frames,
-        radial,
-        edge_source[None],
-        edge_target[None],
-        edge_valid[None],
-    )
+    indices = (edge_source[None], edge_target[None], edge_valid[None])
     planes = (comps, channels, edges)
     bands = (degrees, channels, edges)
     common = [
@@ -309,39 +321,55 @@
         first_kernel(group, zero_rows, scale, *refs)
 
     lines = degrees * block + 8
-    (sent,) = call(
-        first,
-        [jax.ShapeDtypeStruct((group, lines, channels), BF16)],
-        common + [pltpu.VMEM(bands, BF16), pltpu.VMEM(bands, BF16)],
-        10**9,
-        *edge_args,
+    first_args = (
         atom_types[None],
         dataset[None],
         type_table,
         dataset_table,
         router_weight.T,
+        *indices,
+        feats,
+        cot,
+        frames,
+        radial,
+    )
+    (sent,) = call(
+        first,
+        [jax.ShapeDtypeStruct((group, lines, channels), BF16)],
+        [pltpu.VMEM(a.shape, a.dtype) for a in first_args]
+        + common
+        + [pltpu.VMEM(bands, BF16), pltpu.VMEM(bands, BF16), pltpu.SemaphoreType.DMA((len(first_args),))],
+        10**9,
+        *first_args,
+        space=pl.ANY,
+        limit=60 * 1024,
     )
     received = lax.all_to_all(sent, "shard", 0, 0, tiled=True)
 
-    def second(*refs):
-        second_kernel(expert_count, *refs)
-
-    shares, sums = call(
-        second,
-        [
-            jax.ShapeDtypeStruct((group, block, width), BF16),
-            jax.ShapeDtypeStruct((replicas, block, width), BF16),
-        ],
+    def sums_of(*refs):
+        sums_kernel(expert_count, block, order, *refs)
+
+    def shares_of(*refs):
+        shares_kernel(block, *refs)
+
+    columns, cores = lax.axis_size("x"), lax.axis_size("core")
+    line = columns * cores
+    piece = -(-expert_count // line) * block
+    order = [core * columns + column for column in range(columns) for core in range(cores)]
+    (sums,) = call(sums_of, [jax.ShapeDtypeStruct((line, piece, width), BF16)], [], 10**9, received)
+    (shares,) = call(
+        shares_of,
+        [jax.ShapeDtypeStruct((group * block, width), BF16)],
         [],
         10**9,
         received,
         experts.reshape(expert_count * block, width),
     )
-    merged = lax.all_to_all(shares, "shard", 0, 0, tiled=True).reshape(group * block, width)
-    parts = lax.all_to_all(sums, "replica", 0, 0, tiled=True)
-    (own,) = call(sum_kernel, [jax.ShapeDtypeStruct(parts.shape, BF16)], [], 10**7, parts)
-    whole = lax.all_to_all(own, "replica", 0, 0, tiled=True)
-    expert_grad = whole[:expert_count].astype(F32)
+    parts = lax.all_to_all(sums, ("x", "core"), 0, 0, tiled=True)
+    (own,) = call(sum_kernel, [jax.ShapeDtypeStruct((piece, width), BF16)], [], 10**7, parts)
+    merged = lax.all_to_all(shares.reshape(group, block, width), "shard", 0, 0, tiled=True)
+    own = summed_over_pairs(own, "y", columns)
+    whole = lax.all_to_all(own, "x", 0, 0, tiled=True)
 
     def layer(*refs):
         layer_kernel(zero_rows, scale, *refs)
@@ -357,14 +385,24 @@
             pltpu.VMEM(bands, BF16),
         ],
         5 * 10**9,
-        *edge_args,
-        merged,
-    )
+        feats,
+        cot,
+        frames,
+        radial,
+        *indices,
+        merged.reshape(group * block, width),
+    )
+    whole = lax.all_gather(whole.reshape(-1, block, width), "core", axis=0, tiled=True)
+    expert_grad = whole[:expert_count].astype(F32)
     return (updated.transpose(1, 0, 2), feats_grad.transpose(1, 0, 2), expert_grad)
 
 
 def solution(mesh):
-    both = ("shard", "replica")
+    shard_size, replica_size = mesh.devices.shape
+    if math.prod(REPLICA_SIZES) != replica_size:
+        raise ValueError("replica sizes")
+    fine = Mesh(mesh.devices.reshape(shard_size, *REPLICA_SIZES), ("shard", "x", "y", "core"))
+    both = ("shard", "x", "y", "core")
     in_specs = (
         P(both, None, None),
         P(both, None, None),
@@ -381,4 +419,4 @@
         P(None, "shard", None),
     )
     out_specs = (P(both, None, None), P(both, None, None), P(None, "shard", None))
-    return jax.shard_map(shards, mesh=mesh, in_specs=in_specs, out_specs=out_specs, check_vma=False)
+    return jax.shard_map(shards, mesh=fine, in_specs=in_specs, out_specs=out_specs, check_vma=False)

time: 117 us -> 104 us (0.89)
  the two profiles are of different devices: /device:TPU:1 before, /device:TPU:56 now
where the time goes in v2:
time: 104 us; the launch traced here: 103 us
  blocking collectives  50.1 us (48%)
  waiting for transfers between devices  23.2 us (22%)
  starting transfers between devices  15 us (14%)
  Pallas kernels  12.8 us (12%)
  between operations  1.41 us (1%)
    all_to_all x1, blocking collectives, shards(): received = lax.all_to_all(sent, 'shard', 0, 0, tiled=True)  35 us
    all_to_all x1, blocking collectives, shards(): parts = lax.all_to_all(sums, ('x', 'core'), 0, 0, tiled=True)  13 us
    pallas_call x7, Pallas kernels, call(): pl.pallas_call(kernel, out_shape=outs, in_specs=[pl.BlockSpec(memory_spac...  12.8 us
    all_to_all x1, waiting for transfers between devices, shards(): lax.all_to_all(shares.reshape(group, block, width), 'shard', 0, 0, tiled=...  10.5 us
    ppermute x2, waiting for transfers between devices, summed_over_pairs(): other = lax.ppermute(rows, axis, [(i, i ^ turn) for i in range(size)])  8.67 us
    ppermute x2, starting transfers between devices, summed_over_pairs(): other = lax.ppermute(rows, axis, [(i, i ^ turn) for i in range(size)])  6.64 us
    all_to_all x1, starting transfers between devices, shards(): lax.all_to_all(shares.reshape(group, block, width), 'shard', 0, 0, tiled=...  5.03 us
    all_to_all x1, waiting for transfers between devices, shards(): whole = lax.all_to_all(own, 'x', 0, 0, tiled=True)  4.03 us
  transfers between devices with their start and end apart: 4, of which 4 were waited for; matrix products, arithmetic and copies ran while one was open for 1% of the time, Pallas kernels for 2%

profile of v2, /device:TPU:56, one launch (start us, length us, event | category | flops | bytes accessed | tf_op | source)
XLA Modules:
  0.0 103.5 jit_solution(3358106777566366903)
XLA Ops:
  1.3 3.5 %shard_map.148 = bf16[24,56,128]{2,1,0:T(8,128)(2,1)} custom-call(s32[1,64]{1,0:T(1,128)} %bitcast.29, s32[1,1]{1,0:T(1,128)} %bitcast.14.refs_1_, f32[100,128]{1,0:T(8,128)} %refs_2_.2, f32[5,128]{1,0:T(8,128)} %refs_3_.2, f32[28,128]{1,0:T(8,128)} %bitcast.28, s32[1,256]{1,0:T(1,128)} %bitcast.21, s32[1,256]{1,0:T(1,128)} %bitcast.23, s32[1,256]{1,0:T(1,128)} %bitcast.25, ...), custom_call_target="tpu_custom_call" | custom-call | flops 1000000000 | bytes 817412 | tf_op jit(solution)/shard_map/pallas_call | solution.py:266
  4.7 35.0 %all_to_all.20.refs_0_ = bf16[24,56,128]{2,1,0:T(8,128)(2,1)S(1)} all-to-all(bf16[24,56,128]{2,1,0:T(8,128)(2,1)} %shard_map.148), channel_id=1, replica_groups=mesh['shard'=24,'x'=4,'y'=4,'core'=2] {'shard'}, dimensions={0} | all-to-all | bytes 688128 | tf_op jit(solution)/shard_map/all_to_all | solution.py:347
  39.7 1.2 %shard_map.151 = bf16[8,64,384]{2,1,0:T(8,128)(2,1)S(1)} custom-call(bf16[24,56,128]{2,1,0:T(8,128)(2,1)S(1)} %all_to_all.20.refs_0_), custom_call_target="tpu_custom_call" | custom-call | flops 1000000000 | bytes 737280 | tf_op jit(solution)/shard_map/pallas_call | solution.py:266
  40.9 13.0 %all_to_all.21.parts_ref = bf16[8,64,384]{2,1,0:T(8,128)(2,1)S(1)} all-to-all(bf16[8,64,384]{2,1,0:T(8,128)(2,1)S(1)} %shard_map.151), channel_id=1, replica_groups=mesh['shard'=24,'x'=4,'y'=4,'core'=2] {'x','core'}, dimensions={0} | all-to-all | bytes 786432 | tf_op jit(solution)/shard_map/all_to_all | solution.py:368
  53.9 0.1 shard_map.152.own_ref
  54.0 4.0 %collective-permute-start = (bf16[64,384]{1,0:T(8,128)(2,1)S(1)}, bf16[64,384]{1,0:T(8,128)(2,1)S(1)}, u32[]{:S(2)}, u32[]{:S(2)}) collective-permute-start(bf16[64,384]{1,0:T(8,128)(2,1)S(1)} %shard_map.152.own_ref), channel_id=1, source_target_pairs={{0,2},{2,0},{4,6},{6,4},{1,3},{3,1},{5,7},{7,5},{8,10},{10,8},{12,... | collective-permute-start | bytes 147464 | tf_op jit(solution)/shard_map/ppermute | solution.py:280
  58.0 3.1 %collective-permute-done.other_ref = bf16[64,384]{1,0:T(8,128)(2,1)S(1)} collective-permute-done((bf16[64,384]{1,0:T(8,128)(2,1)S(1)}, bf16[64,384]{1,0:T(8,128)(2,1)S(1)}, u32[]{:S(2)}, u32[]{:S(2)}) %collective-permute-start) | collective-permute-done | bytes 49184 | tf_op jit(solution)/shard_map/ppermute | solution.py:280
  61.1 0.0 copy-start
  61.1 2.6 %collective-permute-start.1 = (bf16[64,384]{1,0:T(8,128)(2,1)S(1)}, bf16[64,384]{1,0:T(8,128)(2,1)S(1)}, u32[]{:S(2)}, u32[]{:S(2)}) collective-permute-start(bf16[64,384]{1,0:T(8,128)(2,1)S(1)} %shard_map.153.own_ref), channel_id=1, source_target_pairs={{0,6},{2,4},{4,2},{6,0},{1,7},{3,5},{5,3},{7,1},{8,14},{10,12},{12... | collective-permute-start | bytes 147464 | tf_op jit(solution)/shard_map/ppermute | solution.py:280
  63.7 5.6 %collective-permute-done.1.other_ref = bf16[64,384]{1,0:T(8,128)(2,1)S(1)} collective-permute-done((bf16[64,384]{1,0:T(8,128)(2,1)S(1)}, bf16[64,384]{1,0:T(8,128)(2,1)S(1)}, u32[]{:S(2)}, u32[]{:S(2)}) %collective-permute-start.1) | collective-permute-done | bytes 49184 | tf_op jit(solution)/shard_map/ppermute | solution.py:280
  69.3 0.7 shard_map.154
  70.0 3.4 %all-to-all-start.3 = ((bf16[4,64,384]{2,1,0:T(8,128)(2,1)}), bf16[4,64,384]{2,1,0:T(8,128)(2,1)S(1)}, u32[]{:S(2)}, u32[]{:S(2)}) async-start(bf16[4,64,384]{2,1,0:T(8,128)(2,1)} %shard_map.154), calls=%async_computation.3 | async-start | bytes 393216 | tf_op jit(solution)/shard_map/all_to_all | solution.py:372
  73.4 0.0 copy-done
  73.4 2.3 %shard_map.149 = bf16[384,384]{1,0:T(8,128)(2,1)} custom-call(bf16[24,56,128]{2,1,0:T(8,128)(2,1)S(1)} %all_to_all.20.refs_0_, bf16[448,384]{1,0:T(8,128)(2,1)S(1)} %bitcast.16), custom_call_target="tpu_custom_call" | custom-call | flops 1000000000 | bytes 983040 | tf_op jit(solution)/shard_map/pallas_call | solution.py:266
  75.7 4.0 %all-to-all-done.3 = bf16[4,64,384]{2,1,0:T(8,128)(2,1)S(1)} async-done(((bf16[4,64,384]{2,1,0:T(8,128)(2,1)}), bf16[4,64,384]{2,1,0:T(8,128)(2,1)S(1)}, u32[]{:S(2)}, u32[]{:S(2)}) %all-to-all-start.3) | async-done | bytes 196640 | tf_op jit(solution)/shard_map/all_to_all | solution.py:372
  79.7 5.0 %all-to-all-start.1 = ((bf16[24,16,384]{2,1,0:T(8,128)(2,1)}), bf16[24,16,384]{2,1,0:T(8,128)(2,1)S(1)}, u32[]{:S(2)}, u32[]{:S(2)}) async-start(bf16[24,16,384]{2,1,0:T(8,128)(2,1)} %bitcast.9), calls=%async_computation.1 | async-start | bytes 589824 | tf_op jit(solution)/shard_map/all_to_all | solution.py:370
  84.7 2.1 %all_gather.3 = bf16[32,16,384]{2,1,0:T(8,128)(2,1)S(1)} all-gather(bf16[16,16,384]{2,1,0:T(8,128)(2,1)S(1)} %bitcast.27), channel_id=1, replica_groups=mesh['shard'=24,'x'=4,'y'=4,'core'=2] {'core'}, dimensions={0}, use_global_device_ids=true | all-gather | bytes 589824 | tf_op jit(solution)/shard_map/all_gather | solution.py:395
  86.8 0.0 copy-start.1
  86.8 0.0 copy-start.2
  86.8 0.0 copy-start.3
  86.8 0.0 copy-start.6
  86.9 0.0 copy-start.7
  86.9 0.9 slice_convert_fusion
  87.8 10.5 %all-to-all-done.1 = bf16[24,16,384]{2,1,0:T(8,128)(2,1)S(1)} async-done(((bf16[24,16,384]{2,1,0:T(8,128)(2,1)}), bf16[24,16,384]{2,1,0:T(8,128)(2,1)S(1)}, u32[]{:S(2)}, u32[]{:S(2)}) %all-to-all-start.1) | async-done | bytes 294944 | tf_op jit(solution)/shard_map/all_to_all | solution.py:370
  98.3 0.0 copy-done.1
  98.3 0.0 copy-done.2
  98.3 0.0 copy-done.3
  98.3 0.0 copy-done.4
  98.3 0.0 copy-done.6
  98.3 0.0 copy-done.7
  98.3 0.0 copy-done.5
  98.3 5.2 %shard_map.150 = (bf16[9,64,128]{2,1,0:T(8,128)(2,1)}, f32[9,64,128]{2,1,0:T(8,128)}) custom-call(bf16[9,64,128]{2,1,0:T(8,128)(2,1)S(1)} %bitcast.18, bf16[9,64,128]{2,1,0:T(8,128)(2,1)S(1)} %bitcast.20, bf16[9,9,256]{2,1,0:T(8,128)(2,1)S(1)} %copy-done.3, bf16[256,128]{1,0:T(8,128)(2,1)S(1)} %copy-done.4, s32[1,256]{1,0:T(1,128)S(1)} %bitcast.22, ...), custom_call_target="tpu_custom_call" | custom-call | flops 5000000000 | bytes 1142272 | tf_op jit(solution)/shard_map/pallas_call | solution.py:266
  (3 shorter events, 0.0 us)
Async XLA Ops:
  54.0 7.1 %collective-permute-start = (bf16[64,384]{1,0:T(8,128)(2,1)S(1)}, bf16[64,384]{1,0:T(8,128)(2,1)S(1)}, u32[]{:S(2)}, u32[]{:S(2)}) collective-permute-start(bf16[64,384]{1,0:T(8,128)(2,1)S(1)} %shard_map.152.own_ref), channel_id=1, source_target_pairs={{0,2},{2,0},{4,6},{6,4},{1,3},{3,1},{5,7},{7,5},{8,10},{10,8},{12,... | collective-permute-start | bytes 147464 | tf_op jit(solution)/shard_map/ppermute | solution.py:280
  61.1 12.3 %copy-start = (bf16[28,16,384]{2,1,0:T(8,128)(2,1)S(1)}, bf16[28,16,384]{2,1,0:T(8,128)(2,1)}, u32[]{:S(2)}) copy-start(bf16[28,16,384]{2,1,0:T(8,128)(2,1)} %param.25) | copy-start | bytes 1032196
  61.1 8.2 %collective-permute-start.1 = (bf16[64,384]{1,0:T(8,128)(2,1)S(1)}, bf16[64,384]{1,0:T(8,128)(2,1)S(1)}, u32[]{:S(2)}, u32[]{:S(2)}) collective-permute-start(bf16[64,384]{1,0:T(8,128)(2,1)S(1)} %shard_map.153.own_ref), channel_id=1, source_target_pairs={{0,6},{2,4},{4,2},{6,0},{1,7},{3,5},{5,3},{7,1},{8,14},{10,12},{12... | collective-permute-start | bytes 147464 | tf_op jit(solution)/shard_map/ppermute | solution.py:280
  70.0 9.7 %all-to-all-start.3 = ((bf16[4,64,384]{2,1,0:T(8,128)(2,1)}), bf16[4,64,384]{2,1,0:T(8,128)(2,1)S(1)}, u32[]{:S(2)}, u32[]{:S(2)}) async-start(bf16[4,64,384]{2,1,0:T(8,128)(2,1)} %shard_map.154), calls=%async_computation.3 | async-start | bytes 393216 | tf_op jit(solution)/shard_map/all_to_all | solution.py:372
  79.7 18.6 %all-to-all-start.1 = ((bf16[24,16,384]{2,1,0:T(8,128)(2,1)}), bf16[24,16,384]{2,1,0:T(8,128)(2,1)S(1)}, u32[]{:S(2)}, u32[]{:S(2)}) async-start(bf16[24,16,384]{2,1,0:T(8,128)(2,1)} %bitcast.9), calls=%async_computation.1 | async-start | bytes 589824 | tf_op jit(solution)/shard_map/all_to_all | solution.py:370
  86.8 11.4 %copy-start.1 = (bf16[64,9,128]{2,0,1:T(8,128)(2,1)S(1)}, bf16[64,9,128]{2,0,1:T(8,128)(2,1)}, u32[]{:S(2)}) copy-start(bf16[64,9,128]{2,0,1:T(8,128)(2,1)} %param.13) | copy-start | bytes 442372
  86.8 11.4 %copy-start.2 = (bf16[64,9,128]{2,0,1:T(8,128)(2,1)S(1)}, bf16[64,9,128]{2,0,1:T(8,128)(2,1)}, u32[]{:S(2)}) copy-start(bf16[64,9,128]{2,0,1:T(8,128)(2,1)} %param.14) | copy-start | bytes 442372
  86.8 11.4 %copy-start.3 = (bf16[9,9,256]{2,1,0:T(8,128)(2,1)S(1)}, bf16[9,9,256]{2,1,0:T(8,128)(2,1)}, u32[]{:S(2)}) copy-start(bf16[9,9,256]{2,1,0:T(8,128)(2,1)} %refs_2_.3) | copy-start | bytes 124420
  86.8 11.4 %copy-start.4 = (bf16[256,128]{1,0:T(8,128)(2,1)S(1)}, bf16[256,128]{1,0:T(8,128)(2,1)}, u32[]{:S(2)}) copy-start(bf16[256,128]{1,0:T(8,128)(2,1)} %refs_3_.3) | copy-start | bytes 196612
  86.8 11.5 %copy-start.6 = (s32[256]{0:T(256)S(1)}, s32[256]{0:T(256)}, u32[]{:S(2)}) copy-start(s32[256]{0:T(256)} %param.18) | copy-start | bytes 3076
  86.9 11.4 %copy-start.7 = (s32[256]{0:T(256)S(1)}, s32[256]{0:T(256)}, u32[]{:S(2)}) copy-start(s32[256]{0:T(256)} %param.19) | copy-start | bytes 3076
  87.8 10.6 %copy-start.5 = (s32[256]{0:T(256)S(1)}, s32[256]{0:T(256)}, u32[]{:S(2)}) copy-start(s32[256]{0:T(256)} %param.17) | copy-start | bytes 3076

commit v3 on v2

--- a/solution.py
+++ b/solution.py
@@ -37,7 +37,7 @@
     return parts
 
 
-def mixture_row(types_ref, dataset_ref, type_table_ref, dataset_table_ref, router_ref):
+def mixture_row(lane, types_ref, dataset_ref, type_table_ref, dataset_table_ref, router_ref):
     table = type_table_ref[...]
     atoms = types_ref.shape[1]
     counts = jnp.sum(one_hot(types_ref[...], table.shape[0]).astype(F32), axis=1, keepdims=True)
@@ -49,7 +49,7 @@
     soft = jnp.maximum(logits, 0.0) + jnp.log1p(jnp.exp(-jnp.abs(logits)))
     mixture = soft / jnp.sum(soft, axis=0, keepdims=True)
     shape = (mixture.shape[0], 128)
-    return jnp.sum(jnp.where(iota(shape, 0) == iota(shape, 1), mixture, 0.0), axis=0, keepdims=True)
+    return jnp.sum(jnp.where(iota(shape, 0) + lane == iota(shape, 1), mixture, 0.0), axis=0, keepdims=True)
 
 
 def spread(feats_ref, cot_ref, source_ref, target_ref, valid_ref, gathered_ref, back_ref, scale):
@@ -75,7 +75,7 @@
     return out
 
 
-def first_kernel(group, zero_rows, scale, *refs):
+def first_kernel(zero_rows, scale, *refs):
     count = 12
     sources, (out_ref,), refs = refs[:count], refs[count : count + 1], refs[count + 1 :]
     inputs, refs = refs[:count], refs[count:]
@@ -89,8 +89,9 @@
     router_args, edge_args = inputs[:5], inputs[5:]
     for copy in copies[:5]:
         copy.wait()
-    row = mixture_row(*router_args)
-    group_lines = out_ref.shape[1]
+    group, columns, block, lanes = out_ref.shape
+    slab = band_ref.shape[0] * band_ref.shape[1] // columns
+    row = mixture_row(slab, *router_args)
     source_ref, target_ref, valid_ref, feats_ref, cot_ref, frames_ref, radial_ref = edge_args
     for copy in copies[5:]:
         copy.wait()
@@ -111,71 +112,77 @@
         return carry
 
     lax.fori_loop(0, channels // CHUNK, chunk, 0)
-    width = len(zero_rows) * channels
     edges = band_ref.shape[2]
-    band = band_ref[...].reshape(width, edges)
-    block = width // group
-    for n in range(len(zero_rows)):
-        grad = dot(band, mixed_ref[n], (1, 1)).astype(BF16)
-        out_ref[:, n * block : (n + 1) * block, :] = grad.reshape(group, block, channels)
-    spare = group_lines - len(zero_rows) * block
+    band = band_ref[...].reshape(-1, edges)
+    mixed = mixed_ref[...].reshape(-1, edges)
     tail = jnp.concatenate(
-        [part.astype(F32) for part in split(row)] + [jnp.zeros((spare - PARTS, channels), F32)], axis=0
-    ).astype(BF16)
-    out_ref[:, len(zero_rows) * block :, :] = jnp.broadcast_to(tail[None], (group, spare, channels))
-
-
-def tail_rows(recv_ref, block):
-    channels = recv_ref.shape[2]
-    lines = recv_ref.shape[1] - recv_ref.shape[1] % block
-    return recv_ref[:, lines:, :].astype(F32), lines // block, channels
-
-
-def sums_kernel(expert_count, block, order, recv_ref, sums_ref):
-    tail, pieces, channels = tail_rows(recv_ref, block)
-    group = recv_ref.shape[0]
-    rows, total_rows = group * block, expert_count * block
-    collect_experts = (iota((total_rows, channels), 0) // block == iota((total_rows, channels), 1)).astype(BF16)
-    collect_systems = (iota((group, rows), 1) // block == iota((group, rows), 0)).astype(BF16)
-    same = iota((total_rows, rows), 0) % block == iota((total_rows, rows), 1) % block
-    weights = []
-    for p in range(2):
-        part = tail[:, p, :].astype(BF16)
-        wide = dot(dot(collect_experts, part, (1, 1)).astype(BF16), collect_systems, (1, 0))
-        weights.append(jnp.where(same, wide, 0.0).astype(BF16))
-    for n in range(pieces):
-        grads = recv_ref[:, n * block : (n + 1) * block, :].reshape(rows, channels)
-        total = (dot(weights[0], grads, (1, 0)) + dot(weights[1], grads, (1, 0))).astype(BF16)
-        piece = sums_ref.shape[1]
-        for member, at in enumerate(order):
-            rows_here = max(0, min(piece, total_rows - at * piece))
-            lanes = slice(n * channels, (n + 1) * channels)
-            if rows_here:
-                sums_ref[member, :rows_here, lanes] = total[at * piece : at * piece + rows_here]
-            if rows_here < piece:
-                sums_ref[member, rows_here:, lanes] = jnp.zeros((piece - rows_here, channels), BF16)
-
-
-def shares_kernel(block, recv_ref, experts_ref, shares_ref):
-    tail, _, channels = tail_rows(recv_ref, block)
-    group = recv_ref.shape[0]
-    total_rows, _ = experts_ref.shape
+        [part.astype(F32) for part in split(row)] + [jnp.zeros((block - PARTS, lanes), F32)], axis=0
+    )
+    for column in range(columns):
+        part = mixed[column * slab : (column + 1) * slab]
+        part = jnp.concatenate([part, jnp.zeros((lanes - slab, edges), BF16)], axis=0)
+        grad = dot(band, part, (1, 1)).reshape(group, block, lanes) + tail[None]
+        out_ref[:, column] = grad.astype(BF16)
+
+
+def packed_rows(recv_ref, count, start, stride):
+    systems, block, lanes = recv_ref.shape
+    shape = (count, systems * block)
+    pick = (iota(shape, 1) == iota(shape, 0) * stride + start).astype(BF16)
+    return dot(pick, recv_ref[...].reshape(systems * block, lanes), (1, 0)).astype(BF16)
+
+
+def sums_kernel(expert_count, lane, recv_ref, own_ref, send_ref):
+    systems, block, lanes = recv_ref.shape
+    rows, total_rows = systems * block, expert_count * block
+    mixtures = packed_rows(recv_ref, systems, 0, block)
+    shape = (total_rows, lanes)
+    collect_experts = (iota(shape, 0) // block + lane == iota(shape, 1)).astype(BF16)
+    shape = (systems, rows)
+    collect_systems = (iota(shape, 1) // block == iota(shape, 0)).astype(BF16)
+    wide = dot(dot(collect_experts, mixtures, (1, 1)).astype(BF16), collect_systems, (1, 0))
+    same = iota((total_rows, 1), 0) % block == iota((1, rows), 1) % block
+    weights = jnp.where(same, wide, 0.0).astype(BF16)
+    total = dot(weights, recv_ref[...].reshape(rows, lanes), (1, 0))
+    half = own_ref.shape[0]
+    first = lax.axis_index("core") == 0
+    own_ref[...] = jnp.where(first, total[:half], total[half:]).astype(BF16)
+    send_ref[...] = jnp.where(first, total[half:], total[:half]).astype(BF16)
+
+
+def shares_kernel(group, lane, recv_ref, experts_ref, shares_ref):
+    systems, block, lanes = recv_ref.shape
+    columns = systems // group
+    total_rows = experts_ref.shape[0]
     rows = group * block
-    spread_systems = (iota((rows, group), 0) // block == iota((rows, group), 1)).astype(BF16)
-    spread_experts = (iota((channels, total_rows), 1) // block == iota((channels, total_rows), 0)).astype(BF16)
-    same = iota((rows, total_rows), 0) % block == iota((rows, total_rows), 1) % block
+    shape = (rows, group)
+    spread_systems = (iota(shape, 0) // block == iota(shape, 1)).astype(BF16)
+    shape = (lanes, total_rows)
+    spread_experts = (iota(shape, 1) // block + lane == iota(shape, 0)).astype(BF16)
+    same = iota((rows, 1), 0) % block == iota((1, total_rows), 1) % block
     experts = experts_ref[...]
+    start = lax.axis_index("x") * block
     shares = None
     for p in range(PARTS):
-        part = tail[:, p, :].astype(BF16)
+        part = packed_rows(recv_ref, group, start + p, columns * block)
         wide = dot(dot(spread_systems, part, (1, 0)).astype(BF16), spread_experts, (1, 0))
         term = dot(jnp.where(same, wide, 0.0).astype(BF16), experts, (1, 0))
         shares = term if shares is None else shares + term
     shares_ref[...] = shares.astype(BF16)
 
 
-def sum_kernel(parts_ref, out_ref):
-    out_ref[...] = jnp.sum(parts_ref[...].astype(F32), axis=0).astype(BF16)
+def join_kernel(slab, parts_ref, out_ref):
+    pieces, half, lanes = parts_ref.shape
+    width = out_ref.shape[1]
+    columns = width // slab
+    shape = (lanes, width)
+    for core in range(pieces // columns):
+        total = None
+        for column in range(columns):
+            place = (iota(shape, 0) < slab) & (iota(shape, 0) + column * slab == iota(shape, 1))
+            term = dot(parts_ref[core * columns + column], place.astype(BF16), (1, 0))
+            total = term if total is None else total + term
+        out_ref[core * half : (core + 1) * half] = total
 
 
 def pair_kernel(own_ref, other_ref, out_ref):
@@ -274,13 +281,16 @@
     )(*args)
 
 
-def summed_over_pairs(rows, axis, copies):
+def summed_over_pairs(axis, own, send, copies):
     size = lax.axis_size(axis)
-    for n, turn in enumerate((1, size - 1)):
-        other = lax.ppermute(rows, axis, [(i, i ^ turn) for i in range(size)])
-        shape = (copies, *rows.shape) if n else rows.shape
-        (rows,) = call(pair_kernel, [jax.ShapeDtypeStruct(shape, BF16)], [], 10**6, rows, other)
-    return rows
+    turns = sorted({1, size - 1})
+    for turn in turns:
+        other = lax.ppermute(send, axis, [(i, i ^ turn) for i in range(size)])
+        last = turn == turns[-1] and copies > 1
+        shape = (copies, *own.shape) if last else own.shape
+        (own,) = call(pair_kernel, [jax.ShapeDtypeStruct(shape, BF16)], [], 10**6, own, other)
+        send = own
+    return own
 
 
 def shards(
@@ -318,9 +328,13 @@
     ]
 
     def first(*refs):
-        first_kernel(group, zero_rows, scale, *refs)
-
-    lines = degrees * block + 8
+        first_kernel(zero_rows, scale, *refs)
+
+    columns, cores = lax.axis_size("x"), lax.axis_size("core")
+    slab = width // columns
+    lanes = 128
+    if slab + expert_count > lanes or slab % 16 or expert_count % cores or width % columns:
+        raise ValueError("sizes")
     first_args = (
         atom_types[None],
         dataset[None],
@@ -335,7 +349,7 @@
     )
     (sent,) = call(
         first,
-        [jax.ShapeDtypeStruct((group, lines, channels), BF16)],
+        [jax.ShapeDtypeStruct((group, columns, block, lanes), BF16)],
         [pltpu.VMEM(a.shape, a.dtype) for a in first_args]
         + common
         + [pltpu.VMEM(bands, BF16), pltpu.VMEM(bands, BF16), pltpu.SemaphoreType.DMA((len(first_args),))],
@@ -344,19 +358,18 @@
         space=pl.ANY,
         limit=60 * 1024,
     )
-    received = lax.all_to_all(sent, "shard", 0, 0, tiled=True)
+    sent = sent.reshape(group * columns, block, lanes)
+    received = lax.all_to_all(sent, ("shard", "x"), 0, 0, tiled=True)
 
     def sums_of(*refs):
-        sums_kernel(expert_count, block, order, *refs)
+        sums_kernel(expert_count, slab, *refs)
 
     def shares_of(*refs):
-        shares_kernel(block, *refs)
-
-    columns, cores = lax.axis_size("x"), lax.axis_size("core")
-    line = columns * cores
-    piece = -(-expert_count // line) * block
-    order = [core * columns + column for column in range(columns) for core in range(cores)]
-    (sums,) = call(sums_of, [jax.ShapeDtypeStruct((line, piece, width), BF16)], [], 10**9, received)
+        shares_kernel(group, slab, *refs)
+
+    half = expert_count // cores * block
+    piece = jax.ShapeDtypeStruct((half, lanes), BF16)
+    own, send = call(sums_of, [piece, piece], [], 10**9, received)
     (shares,) = call(
         shares_of,
         [jax.ShapeDtypeStruct((group * block, width), BF16)],
@@ -365,10 +378,9 @@
         received,
         experts.reshape(expert_count * block, width),
     )
-    parts = lax.all_to_all(sums, ("x", "core"), 0, 0, tiled=True)
-    (own,) = call(sum_kernel, [jax.ShapeDtypeStruct((piece, width), BF16)], [], 10**7, parts)
     merged = lax.all_to_all(shares.reshape(group, block, width), "shard", 0, 0, tiled=True)
-    own = summed_over_pairs(own, "y", columns)
+    own = summed_over_pairs("core", own, send, 1)
+    own = summed_over_pairs("y", own, own, columns)
     whole = lax.all_to_all(own, "x", 0, 0, tiled=True)
 
     def layer(*refs):
@@ -392,8 +404,14 @@
         *indices,
         merged.reshape(group * block, width),
     )
-    whole = lax.all_gather(whole.reshape(-1, block, width), "core", axis=0, tiled=True)
-    expert_grad = whole[:expert_count].astype(F32)
+    whole = lax.all_gather(whole, "core", axis=0, tiled=True)
+
+    def join(*refs):
+        join_kernel(slab, *refs)
+
+    out = jax.ShapeDtypeStruct((expert_count * block, width), F32)
+    (expert_grad,) = call(join, [out], [], 10**8, whole)
+    expert_grad = expert_grad.reshape(expert_count, block, width)
     return (updated.transpose(1, 0, 2), feats_grad.transpose(1, 0, 2), expert_grad)
 
 

time: 104 us -> 102 us (0.981)
  the two profiles are of different devices: /device:TPU:56 before, /device:TPU:40 now
where the time goes in v3:
time: 102 us
  blocking collectives  43.9 us (43%)
  waiting for transfers between devices  24.2 us (24%)
  starting transfers between devices  17.8 us (17%)
  Pallas kernels  14.7 us (14%)
  between operations  1.42 us (1%)
    all_to_all x1, blocking collectives, shards(): received = lax.all_to_all(sent, ('shard', 'x'), 0, 0, tiled=True)  41.7 us
    pallas_call x8, Pallas kernels, call(): pl.pallas_call(kernel, out_shape=outs, in_specs=[pl.BlockSpec(memory_spac...  14.7 us
    all_to_all x1, waiting for transfers between devices, shards(): lax.all_to_all(shares.reshape(group, block, width), 'shard', 0, 0, tiled=...  10.8 us
    ppermute x3, waiting for transfers between devices, summed_over_pairs(): other = lax.ppermute(send, axis, [(i, i ^ turn) for i in range(size)])  9.72 us
    ppermute x3, starting transfers between devices, summed_over_pairs(): other = lax.ppermute(send, axis, [(i, i ^ turn) for i in range(size)])  8.67 us
    all_to_all x1, starting transfers between devices, shards(): lax.all_to_all(shares.reshape(group, block, width), 'shard', 0, 0, tiled=...  5.73 us
    all_to_all x1, waiting for transfers between devices, shards(): whole = lax.all_to_all(own, 'x', 0, 0, tiled=True)  3.69 us
    all_to_all x1, starting transfers between devices, shards(): whole = lax.all_to_all(own, 'x', 0, 0, tiled=True)  3.39 us
  transfers between devices with their start and end apart: 5, of which 5 were waited for; matrix products, arithmetic and copies ran while one was open for 0% of the time, Pallas kernels for 4%

profile of v3, /device:TPU:40, one launch (start us, length us, event | category | flops | bytes accessed | tf_op | source)
XLA Modules:
  0.0 102.0 jit_solution(10330319190730453302)
XLA Ops:
  1.3 3.5 %shard_map.148 = bf16[24,4,16,128]{3,2,1,0:T(8,128)(2,1)} custom-call(s32[1,64]{1,0:T(1,128)} %bitcast.31, s32[1,1]{1,0:T(1,128)} %bitcast.15.refs_1_, f32[100,128]{1,0:T(8,128)} %refs_2_.2, f32[5,128]{1,0:T(8,128)} %refs_3_.2, f32[28,128]{1,0:T(8,128)} %bitcast.30, s32[1,256]{1,0:T(1,128)} %bitcast.22, s32[1,256]{1,0:T(1,128)} %bitcast.24, ...), custom_call_target="tpu_custom_call" | custom-call | flops 1000000000 | bytes 866564 | tf_op jit(solution)/shard_map/pallas_call | solution.py:273
  4.8 41.7 %all_to_all.15.refs_0_ = bf16[96,16,128]{2,1,0:T(8,128)(2,1)S(1)} all-to-all(bf16[96,16,128]{2,1,0:T(8,128)(2,1)} %bitcast.29), channel_id=1, replica_groups=mesh['shard'=24,'x'=4,'y'=4,'core'=2] {'shard','x'}, dimensions={0} | all-to-all | bytes 786432 | tf_op jit(solution)/shard_map/all_to_all | solution.py:362
  46.5 1.2 %shard_map.151 = (bf16[224,128]{1,0:T(8,128)(2,1)S(1)}, bf16[224,128]{1,0:T(8,128)(2,1)S(1)}) custom-call(bf16[96,16,128]{2,1,0:T(8,128)(2,1)S(1)} %all_to_all.15.refs_0_), custom_call_target="tpu_custom_call" | custom-call | flops 1000000000 | bytes 507904 | tf_op jit(solution)/shard_map/pallas_call | solution.py:273
  47.8 1.9 %collective-permute-start = (bf16[224,128]{1,0:T(8,128)(2,1)S(1)}, bf16[224,128]{1,0:T(8,128)(2,1)S(1)}, u32[]{:S(2)}, u32[]{:S(2)}) collective-permute-start(bf16[224,128]{1,0:T(8,128)(2,1)S(1)} %get-tuple-element.10), channel_id=1, source_target_pairs={{0,1},{1,0},{2,3},{3,2},{4,5},{5,4},{6,7},{7,6},{8,9},{9,8},{10,11... | collective-permute-start | bytes 172040 | tf_op jit(solution)/shard_map/ppermute | solution.py:288
  49.7 1.2 %collective-permute-done.other_ref = bf16[224,128]{1,0:T(8,128)(2,1)S(1)} collective-permute-done((bf16[224,128]{1,0:T(8,128)(2,1)S(1)}, bf16[224,128]{1,0:T(8,128)(2,1)S(1)}, u32[]{:S(2)}, u32[]{:S(2)}) %collective-permute-start) | collective-permute-done | bytes 57376 | tf_op jit(solution)/shard_map/ppermute | solution.py:288
  50.9 2.7 %collective-permute-start.1 = (bf16[224,128]{1,0:T(8,128)(2,1)S(1)}, bf16[224,128]{1,0:T(8,128)(2,1)S(1)}, u32[]{:S(2)}, u32[]{:S(2)}) collective-permute-start(bf16[224,128]{1,0:T(8,128)(2,1)S(1)} %shard_map.152.own_ref), channel_id=1, source_target_pairs={{0,2},{2,0},{4,6},{6,4},{1,3},{3,1},{5,7},{7,5},{8,10},{10,8},{12,... | collective-permute-start | bytes 172040 | tf_op jit(solution)/shard_map/ppermute | solution.py:288
  53.6 4.3 %collective-permute-done.1.other_ref = bf16[224,128]{1,0:T(8,128)(2,1)S(1)} collective-permute-done((bf16[224,128]{1,0:T(8,128)(2,1)S(1)}, bf16[224,128]{1,0:T(8,128)(2,1)S(1)}, u32[]{:S(2)}, u32[]{:S(2)}) %collective-permute-start.1) | collective-permute-done | bytes 57376 | tf_op jit(solution)/shard_map/ppermute | solution.py:288
  57.9 0.0 copy-start
  57.9 4.1 %collective-permute-start.2 = (bf16[224,128]{1,0:T(8,128)(2,1)S(1)}, bf16[224,128]{1,0:T(8,128)(2,1)S(1)}, u32[]{:S(2)}, u32[]{:S(2)}) collective-permute-start(bf16[224,128]{1,0:T(8,128)(2,1)S(1)} %shard_map.153.own_ref), channel_id=1, source_target_pairs={{0,6},{2,4},{4,2},{6,0},{1,7},{3,5},{5,3},{7,1},{8,14},{10,12},{12... | collective-permute-start | bytes 172040 | tf_op jit(solution)/shard_map/ppermute | solution.py:288
  62.0 4.2 %collective-permute-done.2.other_ref = bf16[224,128]{1,0:T(8,128)(2,1)S(1)} collective-permute-done((bf16[224,128]{1,0:T(8,128)(2,1)S(1)}, bf16[224,128]{1,0:T(8,128)(2,1)S(1)}, u32[]{:S(2)}, u32[]{:S(2)}) %collective-permute-start.2) | collective-permute-done | bytes 57376 | tf_op jit(solution)/shard_map/ppermute | solution.py:288
  66.2 0.7 shard_map.154
  66.9 3.4 %all-to-all-start.2 = ((bf16[4,224,128]{2,1,0:T(8,128)(2,1)}), bf16[4,224,128]{2,1,0:T(8,128)(2,1)S(1)}, u32[]{:S(2)}, u32[]{:S(2)}) async-start(bf16[4,224,128]{2,1,0:T(8,128)(2,1)} %shard_map.154), calls=%async_computation.2 | async-start | bytes 458752 | tf_op jit(solution)/shard_map/all_to_all | solution.py:384
  70.3 0.0 copy-done
  70.3 2.8 %shard_map.149 = bf16[384,384]{1,0:T(8,128)(2,1)} custom-call(bf16[96,16,128]{2,1,0:T(8,128)(2,1)S(1)} %all_to_all.15.refs_0_, bf16[448,384]{1,0:T(8,128)(2,1)S(1)} %bitcast.17), custom_call_target="tpu_custom_call" | custom-call | flops 1000000000 | bytes 1032192 | tf_op jit(solution)/shard_map/pallas_call | solution.py:273
  73.1 3.7 %all-to-all-done.2 = bf16[4,224,128]{2,1,0:T(8,128)(2,1)S(1)} async-done(((bf16[4,224,128]{2,1,0:T(8,128)(2,1)}), bf16[4,224,128]{2,1,0:T(8,128)(2,1)S(1)}, u32[]{:S(2)}, u32[]{:S(2)}) %all-to-all-start.2) | async-done | bytes 229408 | tf_op jit(solution)/shard_map/all_to_all | solution.py:384
  76.8 5.7 %all-to-all-start.1 = ((bf16[24,16,384]{2,1,0:T(8,128)(2,1)}), bf16[24,16,384]{2,1,0:T(8,128)(2,1)S(1)}, u32[]{:S(2)}, u32[]{:S(2)}) async-start(bf16[24,16,384]{2,1,0:T(8,128)(2,1)} %bitcast.10), calls=%async_computation.1 | async-start | bytes 589824 | tf_op jit(solution)/shard_map/all_to_all | solution.py:381
  82.5 2.1 %all_gather.3.refs_0_ = bf16[8,224,128]{2,1,0:T(8,128)(2,1)S(1)} all-gather(bf16[4,224,128]{2,1,0:T(8,128)(2,1)S(1)} %all-to-all-done.2), channel_id=1, replica_groups=mesh['shard'=24,'x'=4,'y'=4,'core'=2] {'core'}, dimensions={0}, use_global_device_ids=true | all-gather | bytes 688128 | tf_op jit(solution)/shard_map/all_gather | solution.py:407
  84.7 0.0 copy-start.1
  84.7 0.0 copy-start.2
  84.7 0.0 copy-start.3
  84.7 0.0 copy-start.6
  84.7 0.0 copy-start.7
  84.7 1.3 %shard_map.155 = f32[448,384]{1,0:T(8,128)} custom-call(bf16[8,224,128]{2,1,0:T(8,128)(2,1)S(1)} %all_gather.3.refs_0_), custom_call_target="tpu_custom_call" | custom-call | flops 100000000 | bytes 1146880 | tf_op jit(solution)/shard_map/pallas_call | solution.py:273
  86.0 10.8 %all-to-all-done.1 = bf16[24,16,384]{2,1,0:T(8,128)(2,1)S(1)} async-done(((bf16[24,16,384]{2,1,0:T(8,128)(2,1)}), bf16[24,16,384]{2,1,0:T(8,128)(2,1)S(1)}, u32[]{:S(2)}, u32[]{:S(2)}) %all-to-all-start.1) | async-done | bytes 294944 | tf_op jit(solution)/shard_map/all_to_all | solution.py:381
  96.8 0.0 copy-done.1
  96.8 0.0 copy-done.2
  96.8 0.0 copy-done.3
  96.8 0.0 copy-done.4
  96.8 0.0 copy-done.6
  96.8 0.0 copy-done.7
  96.8 0.0 copy-done.5
  96.8 5.2 %shard_map.150 = (bf16[9,64,128]{2,1,0:T(8,128)(2,1)}, f32[9,64,128]{2,1,0:T(8,128)}) custom-call(bf16[9,64,128]{2,1,0:T(8,128)(2,1)S(1)} %bitcast.19, bf16[9,64,128]{2,1,0:T(8,128)(2,1)S(1)} %bitcast.21, bf16[9,9,256]{2,1,0:T(8,128)(2,1)S(1)} %copy-done.3, bf16[256,128]{1,0:T(8,128)(2,1)S(1)} %copy-done.4, s32[1,256]{1,0:T(1,128)S(1)} %bitcast.23, ...), custom_call_target="tpu_custom_call" | custom-call | flops 5000000000 | bytes 1142272 | tf_op jit(solution)/shard_map/pallas_call | solution.py:273
  (4 shorter events, 0.0 us)
Async XLA Ops:
  47.8 3.1 %collective-permute-start = (bf16[224,128]{1,0:T(8,128)(2,1)S(1)}, bf16[224,128]{1,0:T(8,128)(2,1)S(1)}, u32[]{:S(2)}, u32[]{:S(2)}) collective-permute-start(bf16[224,128]{1,0:T(8,128)(2,1)S(1)} %get-tuple-element.10), channel_id=1, source_target_pairs={{0,1},{1,0},{2,3},{3,2},{4,5},{5,4},{6,7},{7,6},{8,9},{9,8},{10,11... | collective-permute-start | bytes 172040 | tf_op jit(solution)/shard_map/ppermute | solution.py:288
  50.9 7.0 %collective-permute-start.1 = (bf16[224,128]{1,0:T(8,128)(2,1)S(1)}, bf16[224,128]{1,0:T(8,128)(2,1)S(1)}, u32[]{:S(2)}, u32[]{:S(2)}) collective-permute-start(bf16[224,128]{1,0:T(8,128)(2,1)S(1)} %shard_map.152.own_ref), channel_id=1, source_target_pairs={{0,2},{2,0},{4,6},{6,4},{1,3},{3,1},{5,7},{7,5},{8,10},{10,8},{12,... | collective-permute-start | bytes 172040 | tf_op jit(solution)/shard_map/ppermute | solution.py:288
  57.9 12.4 %copy-start = (bf16[28,16,384]{2,1,0:T(8,128)(2,1)S(1)}, bf16[28,16,384]{2,1,0:T(8,128)(2,1)}, u32[]{:S(2)}) copy-start(bf16[28,16,384]{2,1,0:T(8,128)(2,1)} %param.25) | copy-start | bytes 1032196
  57.9 8.3 %collective-permute-start.2 = (bf16[224,128]{1,0:T(8,128)(2,1)S(1)}, bf16[224,128]{1,0:T(8,128)(2,1)S(1)}, u32[]{:S(2)}, u32[]{:S(2)}) collective-permute-start(bf16[224,128]{1,0:T(8,128)(2,1)S(1)} %shard_map.153.own_ref), channel_id=1, source_target_pairs={{0,6},{2,4},{4,2},{6,0},{1,7},{3,5},{5,3},{7,1},{8,14},{10,12},{12... | collective-permute-start | bytes 172040 | tf_op jit(solution)/shard_map/ppermute | solution.py:288
  66.9 9.9 %all-to-all-start.2 = ((bf16[4,224,128]{2,1,0:T(8,128)(2,1)}), bf16[4,224,128]{2,1,0:T(8,128)(2,1)S(1)}, u32[]{:S(2)}, u32[]{:S(2)}) async-start(bf16[4,224,128]{2,1,0:T(8,128)(2,1)} %shard_map.154), calls=%async_computation.2 | async-start | bytes 458752 | tf_op jit(solution)/shard_map/all_to_all | solution.py:384
  76.8 20.0 %all-to-all-start.1 = ((bf16[24,16,384]{2,1,0:T(8,128)(2,1)}), bf16[24,16,384]{2,1,0:T(8,128)(2,1)S(1)}, u32[]{:S(2)}, u32[]{:S(2)}) async-start(bf16[24,16,384]{2,1,0:T(8,128)(2,1)} %bitcast.10), calls=%async_computation.1 | async-start | bytes 589824 | tf_op jit(solution)/shard_map/all_to_all | solution.py:381
  84.7 12.1 %copy-start.1 = (bf16[64,9,128]{2,0,1:T(8,128)(2,1)S(1)}, bf16[64,9,128]{2,0,1:T(8,128)(2,1)}, u32[]{:S(2)}) copy-start(bf16[64,9,128]{2,0,1:T(8,128)(2,1)} %param.13) | copy-start | bytes 442372
  84.7 12.1 %copy-start.2 = (bf16[64,9,128]{2,0,1:T(8,128)(2,1)S(1)}, bf16[64,9,128]{2,0,1:T(8,128)(2,1)}, u32[]{:S(2)}) copy-start(bf16[64,9,128]{2,0,1:T(8,128)(2,1)} %param.14) | copy-start | bytes 442372
  84.7 12.1 %copy-start.3 = (bf16[9,9,256]{2,1,0:T(8,128)(2,1)S(1)}, bf16[9,9,256]{2,1,0:T(8,128)(2,1)}, u32[]{:S(2)}) copy-start(bf16[9,9,256]{2,1,0:T(8,128)(2,1)} %refs_2_.3) | copy-start | bytes 124420
  84.7 12.1 %copy-start.4 = (bf16[256,128]{1,0:T(8,128)(2,1)S(1)}, bf16[256,128]{1,0:T(8,128)(2,1)}, u32[]{:S(2)}) copy-start(bf16[256,128]{1,0:T(8,128)(2,1)} %refs_3_.3) | copy-start | bytes 196612
  84.7 12.1 %copy-start.6 = (s32[256]{0:T(256)S(1)}, s32[256]{0:T(256)}, u32[]{:S(2)}) copy-start(s32[256]{0:T(256)} %param.18) | copy-start | bytes 3076
  84.7 12.1 %copy-start.7 = (s32[256]{0:T(256)S(1)}, s32[256]{0:T(256)}, u32[]{:S(2)}) copy-start(s32[256]{0:T(256)} %param.19) | copy-start | bytes 3076
  86.0 10.8 %copy-start.5 = (s32[256]{0:T(256)S(1)}, s32[256]{0:T(256)}, u32[]{:S(2)}) copy-start(s32[256]{0:T(256)} %param.17) | copy-start | bytes 3076

commit v4 on v3

--- a/solution.py
+++ b/solution.py
@@ -12,7 +12,8 @@
 BF16 = jnp.bfloat16
 F32 = jnp.float32
 CHUNK = 16
-PARTS = 3
+PARTS = 2
+STRIP = 32
 REPLICA_SIZES = (4, 4, 2)
 
 
@@ -79,7 +80,7 @@
     count = 12
     sources, (out_ref,), refs = refs[:count], refs[count : count + 1], refs[count + 1 :]
     inputs, refs = refs[:count], refs[count:]
-    frames32_ref, gathered_ref, back_ref, gate_ref, band_ref, mixed_ref, sems = refs
+    frames32_ref, gathered_ref, back_ref, gate_ref, band_ref, mixed_ref, held_ref, sems = refs
     copies = [
         pltpu.make_async_copy(source, target, sems.at[n])
         for n, (source, target) in enumerate(zip(sources, inputs))
@@ -87,14 +88,12 @@
     for copy in copies:
         copy.start()
     router_args, edge_args = inputs[:5], inputs[5:]
-    for copy in copies[:5]:
+    for copy in copies:
         copy.wait()
     group, columns, block, lanes = out_ref.shape
     slab = band_ref.shape[0] * band_ref.shape[1] // columns
     row = mixture_row(slab, *router_args)
     source_ref, target_ref, valid_ref, feats_ref, cot_ref, frames_ref, radial_ref = edge_args
-    for copy in copies[5:]:
-        copy.wait()
     comps, _, channels = feats_ref.shape
     frames32_ref[...] = frames_ref[...].astype(F32)
     gate_ref[...] = radial_ref[...].astype(F32).T
@@ -122,7 +121,11 @@
         part = mixed[column * slab : (column + 1) * slab]
         part = jnp.concatenate([part, jnp.zeros((lanes - slab, edges), BF16)], axis=0)
         grad = dot(band, part, (1, 1)).reshape(group, block, lanes) + tail[None]
-        out_ref[:, column] = grad.astype(BF16)
+        held_ref[column] = grad.astype(BF16)
+        copies.append(pltpu.make_async_copy(held_ref.at[column], out_ref.at[:, column], sems.at[len(copies)]))
+        copies[-1].start()
+    for copy in copies[count:]:
+        copy.wait()
 
 
 def packed_rows(recv_ref, count, start, stride):
@@ -144,45 +147,86 @@
     same = iota((total_rows, 1), 0) % block == iota((1, rows), 1) % block
     weights = jnp.where(same, wide, 0.0).astype(BF16)
     total = dot(weights, recv_ref[...].reshape(rows, lanes), (1, 0))
-    half = own_ref.shape[0]
+    half = total_rows // 2
     first = lax.axis_index("core") == 0
-    own_ref[...] = jnp.where(first, total[:half], total[half:]).astype(BF16)
-    send_ref[...] = jnp.where(first, total[half:], total[:half]).astype(BF16)
-
-
-def shares_kernel(group, lane, recv_ref, experts_ref, shares_ref):
-    systems, block, lanes = recv_ref.shape
-    columns = systems // group
+    own_ref[...] = packed(jnp.where(first, total[:half], total[half:]), lane)
+    send_ref[...] = packed(jnp.where(first, total[half:], total[:half]), lane)
+
+
+def rolled(value, source, target):
+    shift = (target - source) * STRIP % value.shape[1]
+    return pltpu.roll(value, shift, 1) if shift else value
+
+
+def in_strips(strips):
+    lane = iota((1, strips[0].shape[1]), 1) // STRIP
+    out = strips[0]
+    for n, strip in enumerate(strips[1:], 1):
+        out = jnp.where(lane == n, strip, out)
+    return out
+
+
+def packed(value, used):
+    per = value.shape[1] // STRIP
+    rows = value.shape[0] // per
+    groups = [value[g * rows : (g + 1) * rows] for g in range(per)]
+    blocks = [in_strips([rolled(v, b, g) for g, v in enumerate(groups)]) for b in range(used // STRIP)]
+    return jnp.concatenate(blocks, axis=0).astype(BF16)
+
+
+def shares_kernel(lane, recv_ref, experts_ref, shares_ref, held_ref, sems):
+    group, _, block, lanes = recv_ref.shape
     total_rows = experts_ref.shape[0]
-    rows = group * block
-    shape = (rows, group)
-    spread_systems = (iota(shape, 0) // block == iota(shape, 1)).astype(BF16)
+    chunks = sems.shape[0]
+    rows = group * block // chunks
+    tail = recv_ref[:, lax.axis_index("x"), :8, :].astype(F32)
+    parts = [tail[:, p, :].astype(BF16) for p in range(PARTS)]
     shape = (lanes, total_rows)
     spread_experts = (iota(shape, 1) // block + lane == iota(shape, 0)).astype(BF16)
     same = iota((rows, 1), 0) % block == iota((1, total_rows), 1) % block
     experts = experts_ref[...]
-    start = lax.axis_index("x") * block
-    shares = None
-    for p in range(PARTS):
-        part = packed_rows(recv_ref, group, start + p, columns * block)
-        wide = dot(dot(spread_systems, part, (1, 0)).astype(BF16), spread_experts, (1, 0))
-        term = dot(jnp.where(same, wide, 0.0).astype(BF16), experts, (1, 0))
-        shares = term if shares is None else shares + term
-    shares_ref[...] = shares.astype(BF16)
-
-
-def join_kernel(slab, parts_ref, out_ref):
-    pieces, half, lanes = parts_ref.shape
-    width = out_ref.shape[1]
+    wide = [dot(part, spread_experts, (1, 0)).astype(BF16) for part in parts]
+    copies = []
+    for n in range(chunks):
+        at = pl.ds(n * rows, rows)
+        shape = (rows, group)
+        spread_systems = ((iota(shape, 0) + n * rows) // block == iota(shape, 1)).astype(BF16)
+        shares = None
+        for part in wide:
+            mine = jnp.where(same, dot(spread_systems, part, (1, 0)), 0.0).astype(BF16)
+            term = dot(mine, experts, (1, 0))
+            shares = term if shares is None else shares + term
+        held_ref[at, :] = shares.astype(BF16)
+        copies.append(pltpu.make_async_copy(held_ref.at[at, :], shares_ref.at[at, :], sems.at[n]))
+        copies[-1].start()
+    for copy in copies:
+        copy.wait()
+
+
+def join_kernel(slab, parts_ref, out_ref, held_ref, sems):
+    pieces, _, lanes = parts_ref.shape
+    half, width = held_ref.shape[1:]
     columns = width // slab
-    shape = (lanes, width)
+    per = lanes // STRIP
+    used = slab // STRIP
+    rows = half // per
+    copies = []
     for core in range(pieces // columns):
-        total = None
-        for column in range(columns):
-            place = (iota(shape, 0) < slab) & (iota(shape, 0) + column * slab == iota(shape, 1))
-            term = dot(parts_ref[core * columns + column], place.astype(BF16), (1, 0))
-            total = term if total is None else total + term
-        out_ref[core * half : (core + 1) * half] = total
+        strips = [
+            parts_ref[core * columns + column, b * rows : (b + 1) * rows, :].astype(F32)
+            for column in range(columns)
+            for b in range(used)
+        ]
+        for g in range(per):
+            for block in range(width // lanes):
+                chosen = [rolled(strips[block * per + q], g, q) for q in range(per)]
+                held_ref[core, g * rows : (g + 1) * rows, block * lanes : (block + 1) * lanes] = in_strips(chosen)
+        copies.append(
+            pltpu.make_async_copy(held_ref.at[core], out_ref.at[pl.ds(core * half, half), :], sems.at[core])
+        )
+        copies[-1].start()
+    for copy in copies:
+        copy.wait()
 
 
 def pair_kernel(own_ref, other_ref, out_ref):
@@ -268,13 +312,13 @@
         grad_ref[j] = cot_ref[j].astype(F32) + summed.astype(BF16).astype(F32)
 
 
-def call(kernel, outs, scratch, flops, *args, space=pltpu.VMEM, limit=32 * 1024):
+def call(kernel, outs, scratch, flops, *args, space=pltpu.VMEM, out_space=pltpu.VMEM, limit=32 * 1024):
     size = sum(math.prod(a.shape) * a.dtype.itemsize for a in (*args, *outs))
     return pl.pallas_call(
         kernel,
         out_shape=outs,
         in_specs=[pl.BlockSpec(memory_space=space)] * len(args),
-        out_specs=[pl.BlockSpec(memory_space=pltpu.VMEM)] * len(outs),
+        out_specs=[pl.BlockSpec(memory_space=out_space)] * len(outs),
         scratch_shapes=scratch,
         cost_estimate=pl.CostEstimate(flops=flops, bytes_accessed=size, transcendentals=0),
         compiler_params=pltpu.CompilerParams(vmem_limit_bytes=limit * 1024),
@@ -333,7 +377,8 @@
     columns, cores = lax.axis_size("x"), lax.axis_size("core")
     slab = width // columns
     lanes = 128
-    if slab + expert_count > lanes or slab % 16 or expert_count % cores or width % columns:
+    half = expert_count // cores * block
+    if slab + expert_count > lanes or slab % STRIP or cores != 2 or expert_count % cores or half % (8 * lanes // STRIP):
         raise ValueError("sizes")
     first_args = (
         atom_types[None],
@@ -352,10 +397,16 @@
         [jax.ShapeDtypeStruct((group, columns, block, lanes), BF16)],
         [pltpu.VMEM(a.shape, a.dtype) for a in first_args]
         + common
-        + [pltpu.VMEM(bands, BF16), pltpu.VMEM(bands, BF16), pltpu.SemaphoreType.DMA((len(first_args),))],
+        + [
+            pltpu.VMEM(bands, BF16),
+            pltpu.VMEM(bands, BF16),
+            pltpu.VMEM((columns, group, block, lanes), BF16),
+            pltpu.SemaphoreType.DMA((len(first_args) + columns,)),
+        ],
         10**9,
         *first_args,
         space=pl.ANY,
+        out_space=pl.ANY,
         limit=60 * 1024,
     )
     sent = sent.reshape(group * columns, block, lanes)
@@ -365,18 +416,18 @@
         sums_kernel(expert_count, slab, *refs)
 
     def shares_of(*refs):
-        shares_kernel(group, slab, *refs)
-
-    half = expert_count // cores * block
-    piece = jax.ShapeDtypeStruct((half, lanes), BF16)
+        shares_kernel(slab, *refs)
+
+    piece = jax.ShapeDtypeStruct((half * slab // lanes, lanes), BF16)
     own, send = call(sums_of, [piece, piece], [], 10**9, received)
     (shares,) = call(
         shares_of,
         [jax.ShapeDtypeStruct((group * block, width), BF16)],
-        [],
+        [pltpu.VMEM((group * block, width), BF16), pltpu.SemaphoreType.DMA((3,))],
         10**9,
-        received,
+        received.reshape(group, columns, block, lanes),
         experts.reshape(expert_count * block, width),
+        out_space=pl.ANY,
     )
     merged = lax.all_to_all(shares.reshape(group, block, width), "shard", 0, 0, tiled=True)
     own = summed_over_pairs("core", own, send, 1)
@@ -410,7 +461,8 @@
         join_kernel(slab, *refs)
 
     out = jax.ShapeDtypeStruct((expert_count * block, width), F32)
-    (expert_grad,) = call(join, [out], [], 10**8, whole)
+    scratch = [pltpu.VMEM((cores, half, width), F32), pltpu.SemaphoreType.DMA((cores,))]
+    (expert_grad,) = call(join, [out], scratch, 10**8, whole, out_space=pl.ANY)
     expert_grad = expert_grad.reshape(expert_count, block, width)
     return (updated.transpose(1, 0, 2), feats_grad.transpose(1, 0, 2), expert_grad)
 

time: 102 us -> 101 us (level)
  the two profiles are of different devices: /device:TPU:40 before, /device:TPU:8 now
where the time goes in v4:
time: 101 us
  blocking collectives  43.8 us (43%)
  waiting for transfers between devices  21.4 us (21%)
  starting transfers between devices  20.3 us (20%)
  Pallas kernels  13.7 us (14%)
  between operations  1.44 us (1%)
    all_to_all x1, blocking collectives, shards(): received = lax.all_to_all(sent, ('shard', 'x'), 0, 0, tiled=True)  41.7 us
    pallas_call x8, Pallas kernels, call(): pl.pallas_call(kernel, out_shape=outs, in_specs=[pl.BlockSpec(memory_spac...  13.7 us
    ppermute x3, starting transfers between devices, summed_over_pairs(): other = lax.ppermute(send, axis, [(i, i ^ turn) for i in range(size)])  12.2 us
    all_to_all x1, waiting for transfers between devices, shards(): lax.all_to_all(shares.reshape(group, block, width), 'shard', 0, 0, tiled=...  10.7 us
    ppermute x3, waiting for transfers between devices, summed_over_pairs(): other = lax.ppermute(send, axis, [(i, i ^ turn) for i in range(size)])  6.37 us
    all_to_all x1, starting transfers between devices, shards(): lax.all_to_all(shares.reshape(group, block, width), 'shard', 0, 0, tiled=...  4.81 us
    all_to_all x1, waiting for transfers between devices, shards(): whole = lax.all_to_all(own, 'x', 0, 0, tiled=True)  4.23 us
    all_to_all x1, starting transfers between devices, shards(): whole = lax.all_to_all(own, 'x', 0, 0, tiled=True)  3.35 us
  transfers between devices with their start and end apart: 5, of which 5 were waited for; matrix products, arithmetic and copies ran while one was open for 0% of the time, Pallas kernels for 3%

profile of v4, /device:TPU:8, one launch (start us, length us, event | category | flops | bytes accessed | tf_op | source)
XLA Modules:
  0.0 100.6 jit_solution(1075884962909379479)
XLA Ops:
  1.3 3.5 %shard_map.148 = bf16[24,4,16,128]{3,2,1,0:T(8,128)(2,1)} custom-call(s32[1,64]{1,0:T(1,128)} %bitcast.33, s32[1,1]{1,0:T(1,128)} %bitcast.16.refs_1_, f32[100,128]{1,0:T(8,128)} %refs_2_.2, f32[5,128]{1,0:T(8,128)} %refs_3_.2, f32[28,128]{1,0:T(8,128)} %bitcast.32, s32[1,256]{1,0:T(1,128)} %bitcast.24, s32[1,256]{1,0:T(1,128)} %bitcast.26, ...), custom_call_target="tpu_custom_call" | custom-call | flops 1000000000 | bytes 866564 | tf_op jit(solution)/shard_map/pallas_call | solution.py:317
  4.8 41.7 %all_to_all.15.refs_0_ = bf16[96,16,128]{2,1,0:T(8,128)(2,1)S(1)} all-to-all(bf16[96,16,128]{2,1,0:T(8,128)(2,1)} %bitcast.31), channel_id=1, replica_groups=mesh['shard'=24,'x'=4,'y'=4,'core'=2] {'shard','x'}, dimensions={0} | all-to-all | bytes 786432 | tf_op jit(solution)/shard_map/all_to_all | solution.py:413
  46.5 1.3 %shard_map.151 = (bf16[168,128]{1,0:T(8,128)(2,1)S(1)}, bf16[168,128]{1,0:T(8,128)(2,1)S(1)}) custom-call(bf16[96,16,128]{2,1,0:T(8,128)(2,1)S(1)} %all_to_all.15.refs_0_), custom_call_target="tpu_custom_call" | custom-call | flops 1000000000 | bytes 479232 | tf_op jit(solution)/shard_map/pallas_call | solution.py:317
  47.8 1.9 %collective-permute-start = (bf16[168,128]{1,0:T(8,128)(2,1)S(1)}, bf16[168,128]{1,0:T(8,128)(2,1)S(1)}, u32[]{:S(2)}, u32[]{:S(2)}) collective-permute-start(bf16[168,128]{1,0:T(8,128)(2,1)S(1)} %get-tuple-element.10), channel_id=1, source_target_pairs={{0,1},{1,0},{2,3},{3,2},{4,5},{5,4},{6,7},{7,6},{8,9},{9,8},{10,11... | collective-permute-start | bytes 129032 | tf_op jit(solution)/shard_map/ppermute | solution.py:332
  49.7 1.2 %collective-permute-done.other_ref = bf16[168,128]{1,0:T(8,128)(2,1)S(1)} collective-permute-done((bf16[168,128]{1,0:T(8,128)(2,1)S(1)}, bf16[168,128]{1,0:T(8,128)(2,1)S(1)}, u32[]{:S(2)}, u32[]{:S(2)}) %collective-permute-start) | collective-permute-done | bytes 43040 | tf_op jit(solution)/shard_map/ppermute | solution.py:332
  51.0 0.0 copy-start
  51.0 4.6 %collective-permute-start.1 = (bf16[168,128]{1,0:T(8,128)(2,1)S(1)}, bf16[168,128]{1,0:T(8,128)(2,1)S(1)}, u32[]{:S(2)}, u32[]{:S(2)}) collective-permute-start(bf16[168,128]{1,0:T(8,128)(2,1)S(1)} %shard_map.152.own_ref), channel_id=1, source_target_pairs={{0,2},{2,0},{4,6},{6,4},{1,3},{3,1},{5,7},{7,5},{8,10},{10,8},{12,... | collective-permute-start | bytes 129032 | tf_op jit(solution)/shard_map/ppermute | solution.py:332
  55.6 2.3 %collective-permute-done.1.other_ref = bf16[168,128]{1,0:T(8,128)(2,1)S(1)} collective-permute-done((bf16[168,128]{1,0:T(8,128)(2,1)S(1)}, bf16[168,128]{1,0:T(8,128)(2,1)S(1)}, u32[]{:S(2)}, u32[]{:S(2)}) %collective-permute-start.1) | collective-permute-done | bytes 43040 | tf_op jit(solution)/shard_map/ppermute | solution.py:332
  57.9 5.6 %collective-permute-start.2 = (bf16[168,128]{1,0:T(8,128)(2,1)S(1)}, bf16[168,128]{1,0:T(8,128)(2,1)S(1)}, u32[]{:S(2)}, u32[]{:S(2)}) collective-permute-start(bf16[168,128]{1,0:T(8,128)(2,1)S(1)} %shard_map.153.own_ref), channel_id=1, source_target_pairs={{0,6},{2,4},{4,2},{6,0},{1,7},{3,5},{5,3},{7,1},{8,14},{10,12},{12... | collective-permute-start | bytes 129032 | tf_op jit(solution)/shard_map/ppermute | solution.py:332
  63.5 2.9 %collective-permute-done.2.other_ref = bf16[168,128]{1,0:T(8,128)(2,1)S(1)} collective-permute-done((bf16[168,128]{1,0:T(8,128)(2,1)S(1)}, bf16[168,128]{1,0:T(8,128)(2,1)S(1)}, u32[]{:S(2)}, u32[]{:S(2)}) %collective-permute-start.2) | collective-permute-done | bytes 43040 | tf_op jit(solution)/shard_map/ppermute | solution.py:332
  66.4 0.7 shard_map.154
  67.1 3.4 %all-to-all-start.2 = ((bf16[4,168,128]{2,1,0:T(8,128)(2,1)}), bf16[4,168,128]{2,1,0:T(8,128)(2,1)S(1)}, u32[]{:S(2)}, u32[]{:S(2)}) async-start(bf16[4,168,128]{2,1,0:T(8,128)(2,1)} %shard_map.154), calls=%async_computation.2 | async-start | bytes 344064 | tf_op jit(solution)/shard_map/all_to_all | solution.py:435
  70.5 0.0 copy-done
  70.5 1.9 %shard_map.149 = bf16[384,384]{1,0:T(8,128)(2,1)} custom-call(bf16[24,4,16,128]{3,2,1,0:T(8,128)(2,1)S(1)} %bitcast.17, bf16[448,384]{1,0:T(8,128)(2,1)S(1)} %bitcast.19), custom_call_target="tpu_custom_call" | custom-call | flops 1000000000 | bytes 1032192 | tf_op jit(solution)/shard_map/pallas_call | solution.py:317
  72.4 4.2 %all-to-all-done.2 = bf16[4,168,128]{2,1,0:T(8,128)(2,1)S(1)} async-done(((bf16[4,168,128]{2,1,0:T(8,128)(2,1)}), bf16[4,168,128]{2,1,0:T(8,128)(2,1)S(1)}, u32[]{:S(2)}, u32[]{:S(2)}) %all-to-all-start.2) | async-done | bytes 172064 | tf_op jit(solution)/shard_map/all_to_all | solution.py:435
  76.6 4.8 %all-to-all-start.1 = ((bf16[24,16,384]{2,1,0:T(8,128)(2,1)}), bf16[24,16,384]{2,1,0:T(8,128)(2,1)S(1)}, u32[]{:S(2)}, u32[]{:S(2)}) async-start(bf16[24,16,384]{2,1,0:T(8,128)(2,1)} %bitcast.11), calls=%async_computation.1 | async-start | bytes 589824 | tf_op jit(solution)/shard_map/all_to_all | solution.py:432
  81.4 2.1 %all_gather.3.refs_0_ = bf16[8,168,128]{2,1,0:T(8,128)(2,1)S(1)} all-gather(bf16[4,168,128]{2,1,0:T(8,128)(2,1)S(1)} %all-to-all-done.2), channel_id=1, replica_groups=mesh['shard'=24,'x'=4,'y'=4,'core'=2] {'core'}, dimensions={0}, use_global_device_ids=true | all-gather | bytes 516096 | tf_op jit(solution)/shard_map/all_gather | solution.py:458
  83.5 0.0 copy-start.2
  83.5 0.0 copy-start.3
  83.5 0.0 copy-start.6
  83.5 0.0 copy-start.7
  83.5 1.1 %shard_map.155 = f32[448,384]{1,0:T(8,128)} custom-call(bf16[8,168,128]{2,1,0:T(8,128)(2,1)S(1)} %all_gather.3.refs_0_), custom_call_target="tpu_custom_call" | custom-call | flops 100000000 | bytes 1032192 | tf_op jit(solution)/shard_map/pallas_call | solution.py:317
  84.6 0.0 copy-start.5
  84.6 10.7 %all-to-all-done.1 = bf16[24,16,384]{2,1,0:T(8,128)(2,1)S(1)} async-done(((bf16[24,16,384]{2,1,0:T(8,128)(2,1)}), bf16[24,16,384]{2,1,0:T(8,128)(2,1)S(1)}, u32[]{:S(2)}, u32[]{:S(2)}) %all-to-all-start.1) | async-done | bytes 294944 | tf_op jit(solution)/shard_map/all_to_all | solution.py:432
  95.4 0.0 copy-done.1
  95.4 0.0 copy-done.2
  95.4 0.0 copy-done.3
  95.4 0.0 copy-done.4
  95.4 0.0 copy-done.6
  95.4 0.0 copy-done.7
  95.4 0.0 copy-done.5
  95.4 5.2 %shard_map.150 = (bf16[9,64,128]{2,1,0:T(8,128)(2,1)}, f32[9,64,128]{2,1,0:T(8,128)}) custom-call(bf16[9,64,128]{2,1,0:T(8,128)(2,1)S(1)} %bitcast.21, bf16[9,64,128]{2,1,0:T(8,128)(2,1)S(1)} %bitcast.23, bf16[9,9,256]{2,1,0:T(8,128)(2,1)S(1)} %copy-done.3, bf16[256,128]{1,0:T(8,128)(2,1)S(1)} %copy-done.4, s32[1,256]{1,0:T(1,128)S(1)} %bitcast.25, ...), custom_call_target="tpu_custom_call" | custom-call | flops 5000000000 | bytes 1142272 | tf_op jit(solution)/shard_map/pallas_call | solution.py:317
  (4 shorter events, 0.0 us)
Async XLA Ops:
  47.8 3.1 %collective-permute-start = (bf16[168,128]{1,0:T(8,128)(2,1)S(1)}, bf16[168,128]{1,0:T(8,128)(2,1)S(1)}, u32[]{:S(2)}, u32[]{:S(2)}) collective-permute-start(bf16[168,128]{1,0:T(8,128)(2,1)S(1)} %get-tuple-element.10), channel_id=1, source_target_pairs={{0,1},{1,0},{2,3},{3,2},{4,5},{5,4},{6,7},{7,6},{8,9},{9,8},{10,11... | collective-permute-start | bytes 129032 | tf_op jit(solution)/shard_map/ppermute | solution.py:332
  51.0 19.5 %copy-start = (bf16[28,16,384]{2,1,0:T(8,128)(2,1)S(1)}, bf16[28,16,384]{2,1,0:T(8,128)(2,1)}, u32[]{:S(2)}) copy-start(bf16[28,16,384]{2,1,0:T(8,128)(2,1)} %param.25) | copy-start | bytes 1032196
  51.0 6.9 %collective-permute-start.1 = (bf16[168,128]{1,0:T(8,128)(2,1)S(1)}, bf16[168,128]{1,0:T(8,128)(2,1)S(1)}, u32[]{:S(2)}, u32[]{:S(2)}) collective-permute-start(bf16[168,128]{1,0:T(8,128)(2,1)S(1)} %shard_map.152.own_ref), channel_id=1, source_target_pairs={{0,2},{2,0},{4,6},{6,4},{1,3},{3,1},{5,7},{7,5},{8,10},{10,8},{12,... | collective-permute-start | bytes 129032 | tf_op jit(solution)/shard_map/ppermute | solution.py:332
  57.9 8.5 %collective-permute-start.2 = (bf16[168,128]{1,0:T(8,128)(2,1)S(1)}, bf16[168,128]{1,0:T(8,128)(2,1)S(1)}, u32[]{:S(2)}, u32[]{:S(2)}) collective-permute-start(bf16[168,128]{1,0:T(8,128)(2,1)S(1)} %shard_map.153.own_ref), channel_id=1, source_target_pairs={{0,6},{2,4},{4,2},{6,0},{1,7},{3,5},{5,3},{7,1},{8,14},{10,12},{12... | collective-permute-start | bytes 129032 | tf_op jit(solution)/shard_map/ppermute | solution.py:332
  67.1 9.5 %all-to-all-start.2 = ((bf16[4,168,128]{2,1,0:T(8,128)(2,1)}), bf16[4,168,128]{2,1,0:T(8,128)(2,1)S(1)}, u32[]{:S(2)}, u32[]{:S(2)}) async-start(bf16[4,168,128]{2,1,0:T(8,128)(2,1)} %shard_map.154), calls=%async_computation.2 | async-start | bytes 344064 | tf_op jit(solution)/shard_map/all_to_all | solution.py:435
  76.6 18.8 %all-to-all-start.1 = ((bf16[24,16,384]{2,1,0:T(8,128)(2,1)}), bf16[24,16,384]{2,1,0:T(8,128)(2,1)S(1)}, u32[]{:S(2)}, u32[]{:S(2)}) async-start(bf16[24,16,384]{2,1,0:T(8,128)(2,1)} %bitcast.11), calls=%async_computation.1 | async-start | bytes 589824 | tf_op jit(solution)/shard_map/all_to_all | solution.py:432
  83.5 11.9 %copy-start.1 = (bf16[64,9,128]{2,0,1:T(8,128)(2,1)S(1)}, bf16[64,9,128]{2,0,1:T(8,128)(2,1)}, u32[]{:S(2)}) copy-start(bf16[64,9,128]{2,0,1:T(8,128)(2,1)} %param.13) | copy-start | bytes 442372
  83.5 11.9 %copy-start.2 = (bf16[64,9,128]{2,0,1:T(8,128)(2,1)S(1)}, bf16[64,9,128]{2,0,1:T(8,128)(2,1)}, u32[]{:S(2)}) copy-start(bf16[64,9,128]{2,0,1:T(8,128)(2,1)} %param.14) | copy-start | bytes 442372
  83.5 11.9 %copy-start.3 = (bf16[9,9,256]{2,1,0:T(8,128)(2,1)S(1)}, bf16[9,9,256]{2,1,0:T(8,128)(2,1)}, u32[]{:S(2)}) copy-start(bf16[9,9,256]{2,1,0:T(8,128)(2,1)} %refs_2_.3) | copy-start | bytes 124420
  83.5 11.9 %copy-start.4 = (bf16[256,128]{1,0:T(8,128)(2,1)S(1)}, bf16[256,128]{1,0:T(8,128)(2,1)}, u32[]{:S(2)}) copy-start(bf16[256,128]{1,0:T(8,128)(2,1)} %refs_3_.3) | copy-start | bytes 196612
  83.5 11.9 %copy-start.6 = (s32[256]{0:T(256)S(1)}, s32[256]{0:T(256)}, u32[]{:S(2)}) copy-start(s32[256]{0:T(256)} %param.18) | copy-start | bytes 3076
  83.5 11.9 %copy-start.7 = (s32[256]{0:T(256)S(1)}, s32[256]{0:T(256)}, u32[]{:S(2)}) copy-start(s32[256]{0:T(256)} %param.19) | copy-start | bytes 3076
  84.6 10.8 %copy-start.5 = (s32[256]{0:T(256)S(1)}, s32[256]{0:T(256)}, u32[]{:S(2)}) copy-start(s32[256]{0:T(256)} %param.17) | copy-start | bytes 3076

commit v5 on v4

--- a/solution.py
+++ b/solution.py
@@ -13,7 +13,7 @@
 F32 = jnp.float32
 CHUNK = 16
 PARTS = 2
-STRIP = 32
+SUB = 4
 REPLICA_SIZES = (4, 4, 2)
 
 
@@ -23,6 +23,10 @@
 
 def dot(a, b, contract):
     return lax.dot_general(a, b, ((contract[:1], contract[1:]), ((), ())), preferred_element_type=F32)
+
+
+def divided(value, by):
+    return jnp.floor((value.astype(F32) + 0.5) * (1.0 / by)).astype(jnp.int32)
 
 
 def one_hot(index_row, count):
@@ -38,7 +42,7 @@
     return parts
 
 
-def mixture_row(lane, types_ref, dataset_ref, type_table_ref, dataset_table_ref, router_ref):
+def mixture_row(types_ref, dataset_ref, type_table_ref, dataset_table_ref, router_ref):
     table = type_table_ref[...]
     atoms = types_ref.shape[1]
     counts = jnp.sum(one_hot(types_ref[...], table.shape[0]).astype(F32), axis=1, keepdims=True)
@@ -50,7 +54,7 @@
     soft = jnp.maximum(logits, 0.0) + jnp.log1p(jnp.exp(-jnp.abs(logits)))
     mixture = soft / jnp.sum(soft, axis=0, keepdims=True)
     shape = (mixture.shape[0], 128)
-    return jnp.sum(jnp.where(iota(shape, 0) + lane == iota(shape, 1), mixture, 0.0), axis=0, keepdims=True)
+    return jnp.sum(jnp.where(iota(shape, 0) == iota(shape, 1), mixture, 0.0), axis=0, keepdims=True)
 
 
 def spread(feats_ref, cot_ref, source_ref, target_ref, valid_ref, gathered_ref, back_ref, scale):
@@ -90,9 +94,7 @@
     router_args, edge_args = inputs[:5], inputs[5:]
     for copy in copies:
         copy.wait()
-    group, columns, block, lanes = out_ref.shape
-    slab = band_ref.shape[0] * band_ref.shape[1] // columns
-    row = mixture_row(slab, *router_args)
+    row = mixture_row(*router_args)
     source_ref, target_ref, valid_ref, feats_ref, cot_ref, frames_ref, radial_ref = edge_args
     comps, _, channels = feats_ref.shape
     frames32_ref[...] = frames_ref[...].astype(F32)
@@ -113,78 +115,79 @@
     lax.fori_loop(0, channels // CHUNK, chunk, 0)
     edges = band_ref.shape[2]
     band = band_ref[...].reshape(-1, edges)
-    mixed = mixed_ref[...].reshape(-1, edges)
-    tail = jnp.concatenate(
-        [part.astype(F32) for part in split(row)] + [jnp.zeros((block - PARTS, lanes), F32)], axis=0
-    )
-    for column in range(columns):
-        part = mixed[column * slab : (column + 1) * slab]
-        part = jnp.concatenate([part, jnp.zeros((lanes - slab, edges), BF16)], axis=0)
-        grad = dot(band, part, (1, 1)).reshape(group, block, lanes) + tail[None]
-        held_ref[column] = grad.astype(BF16)
-        copies.append(pltpu.make_async_copy(held_ref.at[column], out_ref.at[:, column], sems.at[len(copies)]))
-        copies[-1].start()
+    pieces = len(zero_rows)
+    grads = [dot(band, mixed_ref[n], (1, 1)).astype(BF16) for n in range(pieces)]
+    tail = jnp.concatenate([part.astype(F32) for part in split(row)] + [jnp.zeros((16 - PARTS, channels), F32)], axis=0)
+    tail = tail.astype(BF16)
+    lines = SUB * pieces + PARTS
+    batch = 8
+    rows = batch * lines
+    line = iota((rows, 1), 0)
+    message = divided(line, lines)
+    line = line - message * lines
+    data = SUB * pieces
+    wanted = jnp.where(
+        line < data,
+        batch * SUB * (line // SUB) + SUB * message + line % SUB,
+        batch * data + line - data,
+    )
+    place = (iota((rows, batch * data + 16), 1) == wanted).astype(BF16)
+    steps = band.shape[0] // (batch * SUB)
+    chunk_steps = steps // (sems.shape[0] - count)
+    for step in range(steps):
+        at = slice(step * batch * SUB, (step + 1) * batch * SUB)
+        stack = jnp.concatenate([grad[at] for grad in grads] + [tail], axis=0)
+        held_ref[step * rows : (step + 1) * rows] = dot(place, stack, (1, 0)).astype(BF16)
+        if (step + 1) % chunk_steps == 0:
+            done = pl.ds((step + 1 - chunk_steps) * rows, chunk_steps * rows)
+            copies.append(pltpu.make_async_copy(held_ref.at[done], out_ref.at[done], sems.at[len(copies)]))
+            copies[-1].start()
     for copy in copies[count:]:
         copy.wait()
 
 
-def packed_rows(recv_ref, count, start, stride):
-    systems, block, lanes = recv_ref.shape
-    shape = (count, systems * block)
-    pick = (iota(shape, 1) == iota(shape, 0) * stride + start).astype(BF16)
-    return dot(pick, recv_ref[...].reshape(systems * block, lanes), (1, 0)).astype(BF16)
-
-
-def sums_kernel(expert_count, lane, recv_ref, own_ref, send_ref):
-    systems, block, lanes = recv_ref.shape
-    rows, total_rows = systems * block, expert_count * block
-    mixtures = packed_rows(recv_ref, systems, 0, block)
-    shape = (total_rows, lanes)
-    collect_experts = (iota(shape, 0) // block + lane == iota(shape, 1)).astype(BF16)
-    shape = (systems, rows)
-    collect_systems = (iota(shape, 1) // block == iota(shape, 0)).astype(BF16)
-    wide = dot(dot(collect_experts, mixtures, (1, 1)).astype(BF16), collect_systems, (1, 0))
-    same = iota((total_rows, 1), 0) % block == iota((1, rows), 1) % block
-    weights = jnp.where(same, wide, 0.0).astype(BF16)
-    total = dot(weights, recv_ref[...].reshape(rows, lanes), (1, 0))
-    half = total_rows // 2
+def sums_kernel(expert_count, group, lines, recv_ref, own_ref, send_ref, mine_ref):
+    total_lines, lanes = recv_ref.shape
+    systems = total_lines // lines
+    columns = systems // group
+    data = lines - PARTS
+    rows = expert_count * data
+    values = recv_ref[...]
+    shape = (systems, total_lines)
+    picks = [iota(shape, 1) == iota(shape, 0) * lines + data]
+    shape = (group, total_lines)
+    for p in range(PARTS):
+        start = lax.axis_index("x") * lines + data + p
+        picks.append(iota(shape, 1) == iota(shape, 0) * (columns * lines) + start)
+    picked = dot(jnp.concatenate([pick.astype(F32) for pick in picks], axis=0).astype(BF16), values, (1, 0))
+    mine_ref[...] = picked[systems:]
+    column = iota((1, total_lines), 1)
+    system = divided(column, lines)
+    row = iota((rows, 1), 0)
+    expert = divided(row, data)
+    collect_experts = (iota((rows, lanes), 1) == expert).astype(BF16)
+    collect_systems = (iota((systems, total_lines), 0) == system).astype(BF16)
+    narrow = dot(collect_experts, picked[:systems].astype(BF16), (1, 1)).astype(BF16)
+    same = row - expert * data == column - system * lines
+    weights = jnp.where(same, dot(narrow, collect_systems, (1, 0)), 0.0).astype(BF16)
+    total = dot(weights, values, (1, 0))
+    half = rows // 2
     first = lax.axis_index("core") == 0
-    own_ref[...] = packed(jnp.where(first, total[:half], total[half:]), lane)
-    send_ref[...] = packed(jnp.where(first, total[half:], total[:half]), lane)
-
-
-def rolled(value, source, target):
-    shift = (target - source) * STRIP % value.shape[1]
-    return pltpu.roll(value, shift, 1) if shift else value
-
-
-def in_strips(strips):
-    lane = iota((1, strips[0].shape[1]), 1) // STRIP
-    out = strips[0]
-    for n, strip in enumerate(strips[1:], 1):
-        out = jnp.where(lane == n, strip, out)
-    return out
-
-
-def packed(value, used):
-    per = value.shape[1] // STRIP
-    rows = value.shape[0] // per
-    groups = [value[g * rows : (g + 1) * rows] for g in range(per)]
-    blocks = [in_strips([rolled(v, b, g) for g, v in enumerate(groups)]) for b in range(used // STRIP)]
-    return jnp.concatenate(blocks, axis=0).astype(BF16)
-
-
-def shares_kernel(lane, recv_ref, experts_ref, shares_ref, held_ref, sems):
-    group, _, block, lanes = recv_ref.shape
+    own_ref[...] = jnp.where(first, total[:half], total[half:]).astype(BF16)
+    send_ref[...] = jnp.where(first, total[half:], total[:half]).astype(BF16)
+
+
+def shares_kernel(block, mine_ref, experts_ref, shares_ref, held_ref, sems):
+    group = mine_ref.shape[0] // PARTS
+    lanes = mine_ref.shape[1]
     total_rows = experts_ref.shape[0]
     chunks = sems.shape[0]
     rows = group * block // chunks
-    tail = recv_ref[:, lax.axis_index("x"), :8, :].astype(F32)
-    parts = [tail[:, p, :].astype(BF16) for p in range(PARTS)]
     shape = (lanes, total_rows)
-    spread_experts = (iota(shape, 1) // block + lane == iota(shape, 0)).astype(BF16)
+    spread_experts = (iota(shape, 1) // block == iota(shape, 0)).astype(BF16)
     same = iota((rows, 1), 0) % block == iota((1, total_rows), 1) % block
     experts = experts_ref[...]
+    parts = [mine_ref[p * group : (p + 1) * group, :].astype(BF16) for p in range(PARTS)]
     wide = [dot(part, spread_experts, (1, 0)).astype(BF16) for part in parts]
     copies = []
     for n in range(chunks):
@@ -193,8 +196,8 @@
         spread_systems = ((iota(shape, 0) + n * rows) // block == iota(shape, 1)).astype(BF16)
         shares = None
         for part in wide:
-            mine = jnp.where(same, dot(spread_systems, part, (1, 0)), 0.0).astype(BF16)
-            term = dot(mine, experts, (1, 0))
+            weights = jnp.where(same, dot(spread_systems, part, (1, 0)), 0.0).astype(BF16)
+            term = dot(weights, experts, (1, 0))
             shares = term if shares is None else shares + term
         held_ref[at, :] = shares.astype(BF16)
         copies.append(pltpu.make_async_copy(held_ref.at[at, :], shares_ref.at[at, :], sems.at[n]))
@@ -203,24 +206,30 @@
         copy.wait()
 
 
-def join_kernel(slab, parts_ref, out_ref, held_ref, sems):
-    pieces, _, lanes = parts_ref.shape
-    half, width = held_ref.shape[1:]
-    columns = width // slab
-    per = lanes // STRIP
-    used = slab // STRIP
-    rows = half // per
+def join_kernel(block, parts_ref, out_ref, held_ref, sems):
+    cores, half, width = held_ref.shape
+    columns = block // SUB
+    lanes = parts_ref.shape[2]
+    pieces = width // lanes
+    data = SUB * pieces
+    low = iota((2 * SUB, lanes), 0) < SUB
     copies = []
-    for core in range(pieces // columns):
-        strips = [
-            parts_ref[core * columns + column, b * rows : (b + 1) * rows, :].astype(F32)
-            for column in range(columns)
-            for b in range(used)
-        ]
-        for g in range(per):
-            for block in range(width // lanes):
-                chosen = [rolled(strips[block * per + q], g, q) for q in range(per)]
-                held_ref[core, g * rows : (g + 1) * rows, block * lanes : (block + 1) * lanes] = in_strips(chosen)
+
+    def turned(value, line, place):
+        at = line // (2 * SUB) * 2 * SUB
+        value = value[at : at + 2 * SUB]
+        return value if line - at == place else pltpu.roll(value, SUB, 0)
+
+    for core in range(cores):
+        values = [parts_ref[core * columns + column].astype(F32) for column in range(columns)]
+        for expert in range(half // block):
+            for piece in range(pieces):
+                line = expert * data + piece * SUB
+                for column in range(0, columns, 2):
+                    upper = turned(values[column], line, 0)
+                    lower = turned(values[column + 1], line, SUB)
+                    at = expert * block + column * SUB
+                    held_ref[core, at : at + 2 * SUB, piece * lanes : (piece + 1) * lanes] = jnp.where(low, upper, lower)
         copies.append(
             pltpu.make_async_copy(held_ref.at[core], out_ref.at[pl.ds(core * half, half), :], sems.at[core])
         )
@@ -375,10 +384,12 @@
         first_kernel(zero_rows, scale, *refs)
 
     columns, cores = lax.axis_size("x"), lax.axis_size("core")
-    slab = width // columns
     lanes = 128
     half = expert_count // cores * block
-    if slab + expert_count > lanes or slab % STRIP or cores != 2 or expert_count % cores or half % (8 * lanes // STRIP):
+    data = SUB * width // lanes
+    lines = data + PARTS
+    total_lines = group * columns * lines
+    if SUB * columns != block or expert_count > lanes or lines % 2 or cores != 2 or expert_count * data % 16:
         raise ValueError("sizes")
     first_args = (
         atom_types[None],
@@ -394,14 +405,14 @@
     )
     (sent,) = call(
         first,
-        [jax.ShapeDtypeStruct((group, columns, block, lanes), BF16)],
+        [jax.ShapeDtypeStruct((total_lines, lanes), BF16)],
         [pltpu.VMEM(a.shape, a.dtype) for a in first_args]
         + common
         + [
             pltpu.VMEM(bands, BF16),
             pltpu.VMEM(bands, BF16),
-            pltpu.VMEM((columns, group, block, lanes), BF16),
-            pltpu.SemaphoreType.DMA((len(first_args) + columns,)),
+            pltpu.VMEM((total_lines, lanes), BF16),
+            pltpu.SemaphoreType.DMA((len(first_args) + 4,)),
         ],
         10**9,
         *first_args,
@@ -409,23 +420,25 @@
         out_space=pl.ANY,
         limit=60 * 1024,
     )
-    sent = sent.reshape(group * columns, block, lanes)
-    received = lax.all_to_all(sent, ("shard", "x"), 0, 0, tiled=True)
+    sent = sent.reshape(group * columns, lines // 2, 2, lanes)
+    received = lax.all_to_all(sent, ("shard", "x"), 0, 0, tiled=True).reshape(total_lines, lanes)
 
     def sums_of(*refs):
-        sums_kernel(expert_count, slab, *refs)
+        sums_kernel(expert_count, group, lines, *refs)
 
     def shares_of(*refs):
-        shares_kernel(slab, *refs)
-
-    piece = jax.ShapeDtypeStruct((half * slab // lanes, lanes), BF16)
-    own, send = call(sums_of, [piece, piece], [], 10**9, received)
+        shares_kernel(block, *refs)
+
+    piece = jax.ShapeDtypeStruct((expert_count // cores * data, lanes), BF16)
+    own, send, mine = call(
+        sums_of, [piece, piece, jax.ShapeDtypeStruct((PARTS * group, lanes), F32)], [], 10**9, received
+    )
     (shares,) = call(
         shares_of,
         [jax.ShapeDtypeStruct((group * block, width), BF16)],
         [pltpu.VMEM((group * block, width), BF16), pltpu.SemaphoreType.DMA((3,))],
         10**9,
-        received.reshape(group, columns, block, lanes),
+        mine,
         experts.reshape(expert_count * block, width),
         out_space=pl.ANY,
     )
@@ -458,7 +471,7 @@
     whole = lax.all_gather(whole, "core", axis=0, tiled=True)
 
     def join(*refs):
-        join_kernel(slab, *refs)
+        join_kernel(block, *refs)
 
     out = jax.ShapeDtypeStruct((expert_count * block, width), F32)
     scratch = [pltpu.VMEM((cores, half, width), F32), pltpu.SemaphoreType.DMA((cores,))]

time: 101 us -> 100 us (0.990)
  blocking collectives: 43.8 us -> 42.3 us
    all_to_all x1, blocking collectives: 41.7 us -> 40.3 us  [shards(): lax.all_to_all(sent, ('shard', 'x'), 0, 0, tiled=True)]
where the time goes in v5:
time: 100 us; the launch traced here: 99.8 us
  blocking collectives  42.3 us (42%)
  waiting for transfers between devices  22 us (22%)
  starting transfers between devices  20.4 us (20%)
  Pallas kernels  13.6 us (14%)
  between operations  1.44 us (1%)
    all_to_all x1, blocking collectives, shards(): lax.all_to_all(sent, ('shard', 'x'), 0, 0, tiled=True)  40.3 us
    pallas_call x8, Pallas kernels, call(): pl.pallas_call(kernel, out_shape=outs, in_specs=[pl.BlockSpec(memory_spac...  13.6 us
    ppermute x3, starting transfers between devices, summed_over_pairs(): other = lax.ppermute(send, axis, [(i, i ^ turn) for i in range(size)])  12.1 us
    all_to_all x1, waiting for transfers between devices, shards(): lax.all_to_all(shares.reshape(group, block, width), 'shard', 0, 0, tiled=...  11.3 us
    ppermute x3, waiting for transfers between devices, summed_over_pairs(): other = lax.ppermute(send, axis, [(i, i ^ turn) for i in range(size)])  6.39 us
    all_to_all x1, starting transfers between devices, shards(): lax.all_to_all(shares.reshape(group, block, width), 'shard', 0, 0, tiled=...  4.94 us
    all_to_all x1, waiting for transfers between devices, shards(): whole = lax.all_to_all(own, 'x', 0, 0, tiled=True)  4.27 us
    all_to_all x1, starting transfers between devices, shards(): whole = lax.all_to_all(own, 'x', 0, 0, tiled=True)  3.35 us
  transfers between devices with their start and end apart: 5, of which 5 were waited for; matrix products, arithmetic and copies ran while one was open for 0% of the time, Pallas kernels for 3%

profile of v5, /device:TPU:8, one launch (start us, length us, event | category | flops | bytes accessed | tf_op | source)
XLA Modules:
  0.0 99.8 jit_solution(7747879088888726736)
XLA Ops:
  1.3 3.8 %shard_map.148 = bf16[1344,128]{1,0:T(8,128)(2,1)} custom-call(s32[1,64]{1,0:T(1,128)} %bitcast.33, s32[1,1]{1,0:T(1,128)} %bitcast.16.refs_1_, f32[100,128]{1,0:T(8,128)} %refs_2_.2, f32[5,128]{1,0:T(8,128)} %refs_3_.2, f32[28,128]{1,0:T(8,128)} %bitcast.32, s32[1,256]{1,0:T(1,128)} %bitcast.24, s32[1,256]{1,0:T(1,128)} %bitcast.26, s32[1,256]{1,0:T(1,128)} %bitcast.28, ...), custom_call_target="tpu_custom_call" | custom-call | flops 1000000000 | bytes 817412 | tf_op jit(solution)/shard_map/pallas_call | solution.py:326
  5.1 40.3 %all_to_all.15 = bf16[96,7,2,128]{3,2,1,0:T(2,128)(2,1)S(1)} all-to-all(bf16[96,7,2,128]{3,2,1,0:T(2,128)(2,1)} %bitcast.31), channel_id=1, replica_groups=mesh['shard'=24,'x'=4,'y'=4,'core'=2] {'shard','x'}, dimensions={0} | all-to-all | bytes 688128 | tf_op jit(solution)/shard_map/all_to_all | solution.py:424
  45.4 1.2 %shard_map.149 = (bf16[168,128]{1,0:T(8,128)(2,1)S(1)}, bf16[168,128]{1,0:T(8,128)(2,1)S(1)}, f32[48,128]{1,0:T(8,128)S(1)}) custom-call(bf16[1344,128]{1,0:T(8,128)(2,1)S(1)} %bitcast.17), custom_call_target="tpu_custom_call" | custom-call | flops 1000000000 | bytes 454656 | tf_op jit(solution)/shard_map/pallas_call | solution.py:326
  46.5 1.9 %collective-permute-start = (bf16[168,128]{1,0:T(8,128)(2,1)S(1)}, bf16[168,128]{1,0:T(8,128)(2,1)S(1)}, u32[]{:S(2)}, u32[]{:S(2)}) collective-permute-start(bf16[168,128]{1,0:T(8,128)(2,1)S(1)} %get-tuple-element.12), channel_id=1, source_target_pairs={{0,1},{1,0},{2,3},{3,2},{4,5},{5,4},{6,7},{7,6},{8,9},{9,8},{10,11... | collective-permute-start | bytes 129032 | tf_op jit(solution)/shard_map/ppermute | solution.py:341
  48.5 1.2 %collective-permute-done.other_ref = bf16[168,128]{1,0:T(8,128)(2,1)S(1)} collective-permute-done((bf16[168,128]{1,0:T(8,128)(2,1)S(1)}, bf16[168,128]{1,0:T(8,128)(2,1)S(1)}, u32[]{:S(2)}, u32[]{:S(2)}) %collective-permute-start) | collective-permute-done | bytes 43040 | tf_op jit(solution)/shard_map/ppermute | solution.py:341
  49.7 0.0 copy-start
  49.7 4.6 %collective-permute-start.1 = (bf16[168,128]{1,0:T(8,128)(2,1)S(1)}, bf16[168,128]{1,0:T(8,128)(2,1)S(1)}, u32[]{:S(2)}, u32[]{:S(2)}) collective-permute-start(bf16[168,128]{1,0:T(8,128)(2,1)S(1)} %shard_map.152.own_ref), channel_id=1, source_target_pairs={{0,2},{2,0},{4,6},{6,4},{1,3},{3,1},{5,7},{7,5},{8,10},{10,8},{12,... | collective-permute-start | bytes 129032 | tf_op jit(solution)/shard_map/ppermute | solution.py:341
  54.3 2.3 %collective-permute-done.1.other_ref = bf16[168,128]{1,0:T(8,128)(2,1)S(1)} collective-permute-done((bf16[168,128]{1,0:T(8,128)(2,1)S(1)}, bf16[168,128]{1,0:T(8,128)(2,1)S(1)}, u32[]{:S(2)}, u32[]{:S(2)}) %collective-permute-start.1) | collective-permute-done | bytes 43040 | tf_op jit(solution)/shard_map/ppermute | solution.py:341
  56.6 5.6 %collective-permute-start.2 = (bf16[168,128]{1,0:T(8,128)(2,1)S(1)}, bf16[168,128]{1,0:T(8,128)(2,1)S(1)}, u32[]{:S(2)}, u32[]{:S(2)}) collective-permute-start(bf16[168,128]{1,0:T(8,128)(2,1)S(1)} %shard_map.153.own_ref), channel_id=1, source_target_pairs={{0,6},{2,4},{4,2},{6,0},{1,7},{3,5},{5,3},{7,1},{8,14},{10,12},{12... | collective-permute-start | bytes 129032 | tf_op jit(solution)/shard_map/ppermute | solution.py:341
  62.3 2.9 %collective-permute-done.2.other_ref = bf16[168,128]{1,0:T(8,128)(2,1)S(1)} collective-permute-done((bf16[168,128]{1,0:T(8,128)(2,1)S(1)}, bf16[168,128]{1,0:T(8,128)(2,1)S(1)}, u32[]{:S(2)}, u32[]{:S(2)}) %collective-permute-start.2) | collective-permute-done | bytes 43040 | tf_op jit(solution)/shard_map/ppermute | solution.py:341
  65.1 0.7 shard_map.154
  65.8 3.4 %all-to-all-start.2 = ((bf16[4,168,128]{2,1,0:T(8,128)(2,1)}), bf16[4,168,128]{2,1,0:T(8,128)(2,1)S(1)}, u32[]{:S(2)}, u32[]{:S(2)}) async-start(bf16[4,168,128]{2,1,0:T(8,128)(2,1)} %shard_map.154), calls=%async_computation.2 | async-start | bytes 344064 | tf_op jit(solution)/shard_map/all_to_all | solution.py:448
  69.2 0.0 copy-done
  69.2 1.9 %shard_map.150 = bf16[384,384]{1,0:T(8,128)(2,1)} custom-call(f32[48,128]{1,0:T(8,128)S(1)} %get-tuple-element.8.refs_0_, bf16[448,384]{1,0:T(8,128)(2,1)S(1)} %bitcast.19), custom_call_target="tpu_custom_call" | custom-call | flops 1000000000 | bytes 663552 | tf_op jit(solution)/shard_map/pallas_call | solution.py:326
  71.1 4.3 %all-to-all-done.2 = bf16[4,168,128]{2,1,0:T(8,128)(2,1)S(1)} async-done(((bf16[4,168,128]{2,1,0:T(8,128)(2,1)}), bf16[4,168,128]{2,1,0:T(8,128)(2,1)S(1)}, u32[]{:S(2)}, u32[]{:S(2)}) %all-to-all-start.2) | async-done | bytes 172064 | tf_op jit(solution)/shard_map/all_to_all | solution.py:448
  75.3 4.9 %all-to-all-start.1 = ((bf16[24,16,384]{2,1,0:T(8,128)(2,1)}), bf16[24,16,384]{2,1,0:T(8,128)(2,1)S(1)}, u32[]{:S(2)}, u32[]{:S(2)}) async-start(bf16[24,16,384]{2,1,0:T(8,128)(2,1)} %bitcast.11), calls=%async_computation.1 | async-start | bytes 589824 | tf_op jit(solution)/shard_map/all_to_all | solution.py:445
  80.3 2.1 %all_gather.3.refs_0_ = bf16[8,168,128]{2,1,0:T(8,128)(2,1)S(1)} all-gather(bf16[4,168,128]{2,1,0:T(8,128)(2,1)S(1)} %all-to-all-done.2), channel_id=1, replica_groups=mesh['shard'=24,'x'=4,'y'=4,'core'=2] {'core'}, dimensions={0}, use_global_device_ids=true | all-gather | bytes 516096 | tf_op jit(solution)/shard_map/all_gather | solution.py:471
  82.3 0.0 copy-start.1
  82.3 0.0 copy-start.2
  82.4 0.0 copy-start.6
  82.4 0.0 copy-start.7
  82.4 0.9 shard_map.155
  83.3 0.0 copy-start.5
  83.3 11.3 %all-to-all-done.1 = bf16[24,16,384]{2,1,0:T(8,128)(2,1)S(1)} async-done(((bf16[24,16,384]{2,1,0:T(8,128)(2,1)}), bf16[24,16,384]{2,1,0:T(8,128)(2,1)S(1)}, u32[]{:S(2)}, u32[]{:S(2)}) %all-to-all-start.1) | async-done | bytes 294944 | tf_op jit(solution)/shard_map/all_to_all | solution.py:445
  94.6 0.0 copy-done.1
  94.6 0.0 copy-done.2
  94.6 0.0 copy-done.3
  94.6 0.0 copy-done.4
  94.6 0.0 copy-done.6
  94.6 0.0 copy-done.7
  94.7 0.0 copy-done.5
  94.7 5.2 %shard_map.151 = (bf16[9,64,128]{2,1,0:T(8,128)(2,1)}, f32[9,64,128]{2,1,0:T(8,128)}) custom-call(bf16[9,64,128]{2,1,0:T(8,128)(2,1)S(1)} %bitcast.21, bf16[9,64,128]{2,1,0:T(8,128)(2,1)S(1)} %bitcast.23, bf16[9,9,256]{2,1,0:T(8,128)(2,1)S(1)} %copy-done.3, bf16[256,128]{1,0:T(8,128)(2,1)S(1)} %copy-done.4, s32[1,256]{1,0:T(1,128)S(1)} %bitcast.25, ...), custom_call_target="tpu_custom_call" | custom-call | flops 5000000000 | bytes 1142272 | tf_op jit(solution)/shard_map/pallas_call | solution.py:326
  (4 shorter events, 0.0 us)
Async XLA Ops:
  46.5 3.1 %collective-permute-start = (bf16[168,128]{1,0:T(8,128)(2,1)S(1)}, bf16[168,128]{1,0:T(8,128)(2,1)S(1)}, u32[]{:S(2)}, u32[]{:S(2)}) collective-permute-start(bf16[168,128]{1,0:T(8,128)(2,1)S(1)} %get-tuple-element.12), channel_id=1, source_target_pairs={{0,1},{1,0},{2,3},{3,2},{4,5},{5,4},{6,7},{7,6},{8,9},{9,8},{10,11... | collective-permute-start | bytes 129032 | tf_op jit(solution)/shard_map/ppermute | solution.py:341
  49.7 19.5 %copy-start = (bf16[28,16,384]{2,1,0:T(8,128)(2,1)S(1)}, bf16[28,16,384]{2,1,0:T(8,128)(2,1)}, u32[]{:S(2)}) copy-start(bf16[28,16,384]{2,1,0:T(8,128)(2,1)} %param.25) | copy-start | bytes 1032196
  49.7 6.9 %collective-permute-start.1 = (bf16[168,128]{1,0:T(8,128)(2,1)S(1)}, bf16[168,128]{1,0:T(8,128)(2,1)S(1)}, u32[]{:S(2)}, u32[]{:S(2)}) collective-permute-start(bf16[168,128]{1,0:T(8,128)(2,1)S(1)} %shard_map.152.own_ref), channel_id=1, source_target_pairs={{0,2},{2,0},{4,6},{6,4},{1,3},{3,1},{5,7},{7,5},{8,10},{10,8},{12,... | collective-permute-start | bytes 129032 | tf_op jit(solution)/shard_map/ppermute | solution.py:341
  56.6 8.5 %collective-permute-start.2 = (bf16[168,128]{1,0:T(8,128)(2,1)S(1)}, bf16[168,128]{1,0:T(8,128)(2,1)S(1)}, u32[]{:S(2)}, u32[]{:S(2)}) collective-permute-start(bf16[168,128]{1,0:T(8,128)(2,1)S(1)} %shard_map.153.own_ref), channel_id=1, source_target_pairs={{0,6},{2,4},{4,2},{6,0},{1,7},{3,5},{5,3},{7,1},{8,14},{10,12},{12... | collective-permute-start | bytes 129032 | tf_op jit(solution)/shard_map/ppermute | solution.py:341
  65.8 9.5 %all-to-all-start.2 = ((bf16[4,168,128]{2,1,0:T(8,128)(2,1)}), bf16[4,168,128]{2,1,0:T(8,128)(2,1)S(1)}, u32[]{:S(2)}, u32[]{:S(2)}) async-start(bf16[4,168,128]{2,1,0:T(8,128)(2,1)} %shard_map.154), calls=%async_computation.2 | async-start | bytes 344064 | tf_op jit(solution)/shard_map/all_to_all | solution.py:448
  75.3 19.3 %all-to-all-start.1 = ((bf16[24,16,384]{2,1,0:T(8,128)(2,1)}), bf16[24,16,384]{2,1,0:T(8,128)(2,1)S(1)}, u32[]{:S(2)}, u32[]{:S(2)}) async-start(bf16[24,16,384]{2,1,0:T(8,128)(2,1)} %bitcast.11), calls=%async_computation.1 | async-start | bytes 589824 | tf_op jit(solution)/shard_map/all_to_all | solution.py:445
  82.3 12.3 %copy-start.1 = (bf16[64,9,128]{2,0,1:T(8,128)(2,1)S(1)}, bf16[64,9,128]{2,0,1:T(8,128)(2,1)}, u32[]{:S(2)}) copy-start(bf16[64,9,128]{2,0,1:T(8,128)(2,1)} %param.13) | copy-start | bytes 442372
  82.3 12.3 %copy-start.2 = (bf16[64,9,128]{2,0,1:T(8,128)(2,1)S(1)}, bf16[64,9,128]{2,0,1:T(8,128)(2,1)}, u32[]{:S(2)}) copy-start(bf16[64,9,128]{2,0,1:T(8,128)(2,1)} %param.14) | copy-start | bytes 442372
  82.3 12.3 %copy-start.3 = (bf16[9,9,256]{2,1,0:T(8,128)(2,1)S(1)}, bf16[9,9,256]{2,1,0:T(8,128)(2,1)}, u32[]{:S(2)}) copy-start(bf16[9,9,256]{2,1,0:T(8,128)(2,1)} %refs_2_.3) | copy-start | bytes 124420
  82.3 12.3 %copy-start.4 = (bf16[256,128]{1,0:T(8,128)(2,1)S(1)}, bf16[256,128]{1,0:T(8,128)(2,1)}, u32[]{:S(2)}) copy-start(bf16[256,128]{1,0:T(8,128)(2,1)} %refs_3_.3) | copy-start | bytes 196612
  82.4 12.3 %copy-start.6 = (s32[256]{0:T(256)S(1)}, s32[256]{0:T(256)}, u32[]{:S(2)}) copy-start(s32[256]{0:T(256)} %param.18) | copy-start | bytes 3076
  82.4 12.3 %copy-start.7 = (s32[256]{0:T(256)S(1)}, s32[256]{0:T(256)}, u32[]{:S(2)}) copy-start(s32[256]{0:T(256)} %param.19) | copy-start | bytes 3076
  83.3 11.4 %copy-start.5 = (s32[256]{0:T(256)S(1)}, s32[256]{0:T(256)}, u32[]{:S(2)}) copy-start(s32[256]{0:T(256)} %param.17) | copy-start | bytes 3076

commit v6 on v5

--- a/solution.py
+++ b/solution.py
@@ -61,7 +61,8 @@
     atoms = feats_ref.shape[1]
     source = one_hot(source_ref[...], atoms).astype(BF16)
     incidence = (one_hot(target_ref[...], atoms) & (valid_ref[...] > 0)).astype(BF16)
-    for j in range(feats_ref.shape[0]):
+    comps = feats_ref.shape[0]
+    for j in range(comps):
         gathered_ref[j] = dot(feats_ref[j], source, (0, 0))
         back_ref[j] = dot(cot_ref[j], incidence, (0, 0)) * scale
     return source, incidence
@@ -92,33 +93,7 @@
     for copy in copies:
         copy.start()
     router_args, edge_args = inputs[:5], inputs[5:]
-    for copy in copies:
-        copy.wait()
-    row = mixture_row(*router_args)
-    source_ref, target_ref, valid_ref, feats_ref, cot_ref, frames_ref, radial_ref = edge_args
-    comps, _, channels = feats_ref.shape
-    frames32_ref[...] = frames_ref[...].astype(F32)
-    gate_ref[...] = radial_ref[...].astype(F32).T
-    spread(feats_ref, cot_ref, source_ref, target_ref, valid_ref, gathered_ref, back_ref, scale)
-
-    def chunk(step, carry):
-        at = pl.ds(pl.multiple_of(step * CHUNK, CHUNK), CHUNK)
-        values = [gathered_ref[j, at, :] for j in range(comps)]
-        for n, total in enumerate(rotate(frames32_ref, zero_rows, values)):
-            band_ref[n, at, :] = total.astype(BF16)
-        values = [back_ref[j, at, :] for j in range(comps)]
-        gate = gate_ref[at, :]
-        for n, total in enumerate(rotate(frames32_ref, zero_rows, values)):
-            mixed_ref[n, at, :] = (total.astype(BF16).astype(F32) * gate).astype(BF16)
-        return carry
-
-    lax.fori_loop(0, channels // CHUNK, chunk, 0)
-    edges = band_ref.shape[2]
-    band = band_ref[...].reshape(-1, edges)
     pieces = len(zero_rows)
-    grads = [dot(band, mixed_ref[n], (1, 1)).astype(BF16) for n in range(pieces)]
-    tail = jnp.concatenate([part.astype(F32) for part in split(row)] + [jnp.zeros((16 - PARTS, channels), F32)], axis=0)
-    tail = tail.astype(BF16)
     lines = SUB * pieces + PARTS
     batch = 8
     rows = batch * lines
@@ -132,6 +107,32 @@
         batch * data + line - data,
     )
     place = (iota((rows, batch * data + 16), 1) == wanted).astype(BF16)
+    for copy in copies:
+        copy.wait()
+    row = mixture_row(*router_args)
+    source_ref, target_ref, valid_ref, feats_ref, cot_ref, frames_ref, radial_ref = edge_args
+    comps, _, channels = feats_ref.shape
+    frames32_ref[...] = frames_ref[...].astype(F32)
+    gate_ref[...] = radial_ref[...].astype(F32).T
+    spread(feats_ref, cot_ref, source_ref, target_ref, valid_ref, gathered_ref, back_ref, scale)
+
+    def chunk(step, carry):
+        at = pl.ds(pl.multiple_of(step * CHUNK, CHUNK), CHUNK)
+        values = [gathered_ref[j, at, :] for j in range(comps)]
+        for n, total in enumerate(rotate(frames32_ref, zero_rows, values)):
+            band_ref[n, at, :] = total.astype(BF16)
+        values = [back_ref[j, at, :] for j in range(comps)]
+        gate = gate_ref[at, :]
+        for n, total in enumerate(rotate(frames32_ref, zero_rows, values)):
+            mixed_ref[n, at, :] = (total.astype(BF16).astype(F32) * gate).astype(BF16)
+        return carry
+
+    lax.fori_loop(0, channels // CHUNK, chunk, 0, unroll=True)
+    edges = band_ref.shape[2]
+    band = band_ref[...].reshape(-1, edges)
+    grads = [dot(band, mixed_ref[n], (1, 1)).astype(BF16) for n in range(pieces)]
+    tail = jnp.concatenate([part.astype(F32) for part in split(row)] + [jnp.zeros((16 - PARTS, channels), F32)], axis=0)
+    tail = tail.astype(BF16)
     steps = band.shape[0] // (batch * SUB)
     chunk_steps = steps // (sems.shape[0] - count)
     for step in range(steps):
@@ -194,11 +195,9 @@
         at = pl.ds(n * rows, rows)
         shape = (rows, group)
         spread_systems = ((iota(shape, 0) + n * rows) // block == iota(shape, 1)).astype(BF16)
-        shares = None
-        for part in wide:
-            weights = jnp.where(same, dot(spread_systems, part, (1, 0)), 0.0).astype(BF16)
-            term = dot(weights, experts, (1, 0))
-            shares = term if shares is None else shares + term
+        weights = [jnp.where(same, dot(spread_systems, part, (1, 0)), 0.0).astype(BF16) for part in wide]
+        terms = dot(jnp.concatenate(weights, axis=0), experts, (1, 0))
+        shares = sum(terms[p * rows : (p + 1) * rows] for p in range(PARTS))
         held_ref[at, :] = shares.astype(BF16)
         copies.append(pltpu.make_async_copy(held_ref.at[at, :], shares_ref.at[at, :], sems.at[n]))
         copies[-1].start()
@@ -436,7 +435,7 @@
     (shares,) = call(
         shares_of,
         [jax.ShapeDtypeStruct((group * block, width), BF16)],
-        [pltpu.VMEM((group * block, width), BF16), pltpu.SemaphoreType.DMA((3,))],
+        [pltpu.VMEM((group * block, width), BF16), pltpu.SemaphoreType.DMA((2,))],
         10**9,
         mine,
         experts.reshape(expert_count * block, width),

time: 100 us -> 100 us (level)
  no operation moved by 1% of the time
where the time goes in v6:
time: 100 us; the launch traced here: 99.6 us
  blocking collectives  42.4 us (42%)
  waiting for transfers between devices  22.2 us (22%)
  starting transfers between devices  20.4 us (20%)
  Pallas kernels  13.1 us (13%)
  between operations  1.44 us (1%)
    all_to_all x1, blocking collectives, shards(): lax.all_to_all(sent, ('shard', 'x'), 0, 0, tiled=True)  40.3 us
    pallas_call x8, Pallas kernels, call(): pl.pallas_call(kernel, out_shape=outs, in_specs=[pl.BlockSpec(memory_spac...  13.1 us
    ppermute x3, starting transfers between devices, summed_over_pairs(): other = lax.ppermute(send, axis, [(i, i ^ turn) for i in range(size)])  12.1 us
    all_to_all x1, waiting for transfers between devices, shards(): lax.all_to_all(shares.reshape(group, block, width), 'shard', 0, 0, tiled=...  11.3 us
    ppermute x3, waiting for transfers between devices, summed_over_pairs(): other = lax.ppermute(send, axis, [(i, i ^ turn) for i in range(size)])  6.4 us
    all_to_all x1, starting transfers between devices, shards(): lax.all_to_all(shares.reshape(group, block, width), 'shard', 0, 0, tiled=...  4.93 us
    all_to_all x1, waiting for transfers between devices, shards(): whole = lax.all_to_all(own, 'x', 0, 0, tiled=True)  4.5 us
    all_to_all x1, starting transfers between devices, shards(): whole = lax.all_to_all(own, 'x', 0, 0, tiled=True)  3.35 us
  transfers between devices with their start and end apart: 5, of which 5 were waited for; matrix products, arithmetic and copies ran while one was open for 0% of the time, Pallas kernels for 3%

profile of v6, /device:TPU:8, one launch (start us, length us, event | category | flops | bytes accessed | tf_op | source)
XLA Modules:
  0.0 99.6 jit_solution(17812087806225135558)
XLA Ops:
  1.3 3.5 %shard_map.148 = bf16[1344,128]{1,0:T(8,128)(2,1)} custom-call(s32[1,64]{1,0:T(1,128)} %bitcast.33, s32[1,1]{1,0:T(1,128)} %bitcast.16.refs_1_, f32[100,128]{1,0:T(8,128)} %refs_2_.2, f32[5,128]{1,0:T(8,128)} %refs_3_.2, f32[28,128]{1,0:T(8,128)} %bitcast.32, s32[1,256]{1,0:T(1,128)} %bitcast.24, s32[1,256]{1,0:T(1,128)} %bitcast.26, s32[1,256]{1,0:T(1,128)} %bitcast.28, ...), custom_call_target="tpu_custom_call" | custom-call | flops 1000000000 | bytes 817412 | tf_op jit(solution)/shard_map/pallas_call | solution.py:325
  4.8 40.3 %all_to_all.15 = bf16[96,7,2,128]{3,2,1,0:T(2,128)(2,1)S(1)} all-to-all(bf16[96,7,2,128]{3,2,1,0:T(2,128)(2,1)} %bitcast.31), channel_id=1, replica_groups=mesh['shard'=24,'x'=4,'y'=4,'core'=2] {'shard','x'}, dimensions={0} | all-to-all | bytes 688128 | tf_op jit(solution)/shard_map/all_to_all | solution.py:423
  45.1 1.2 %shard_map.149 = (bf16[168,128]{1,0:T(8,128)(2,1)S(1)}, bf16[168,128]{1,0:T(8,128)(2,1)S(1)}, f32[48,128]{1,0:T(8,128)S(1)}) custom-call(bf16[1344,128]{1,0:T(8,128)(2,1)S(1)} %bitcast.17), custom_call_target="tpu_custom_call" | custom-call | flops 1000000000 | bytes 454656 | tf_op jit(solution)/shard_map/pallas_call | solution.py:325
  46.3 1.9 %collective-permute-start = (bf16[168,128]{1,0:T(8,128)(2,1)S(1)}, bf16[168,128]{1,0:T(8,128)(2,1)S(1)}, u32[]{:S(2)}, u32[]{:S(2)}) collective-permute-start(bf16[168,128]{1,0:T(8,128)(2,1)S(1)} %get-tuple-element.12), channel_id=1, source_target_pairs={{0,1},{1,0},{2,3},{3,2},{4,5},{5,4},{6,7},{7,6},{8,9},{9,8},{10,11... | collective-permute-start | bytes 129032 | tf_op jit(solution)/shard_map/ppermute | solution.py:340
  48.2 1.2 %collective-permute-done.other_ref = bf16[168,128]{1,0:T(8,128)(2,1)S(1)} collective-permute-done((bf16[168,128]{1,0:T(8,128)(2,1)S(1)}, bf16[168,128]{1,0:T(8,128)(2,1)S(1)}, u32[]{:S(2)}, u32[]{:S(2)}) %collective-permute-start) | collective-permute-done | bytes 43040 | tf_op jit(solution)/shard_map/ppermute | solution.py:340
  49.4 0.0 copy-start
  49.4 4.6 %collective-permute-start.1 = (bf16[168,128]{1,0:T(8,128)(2,1)S(1)}, bf16[168,128]{1,0:T(8,128)(2,1)S(1)}, u32[]{:S(2)}, u32[]{:S(2)}) collective-permute-start(bf16[168,128]{1,0:T(8,128)(2,1)S(1)} %shard_map.152.own_ref), channel_id=1, source_target_pairs={{0,2},{2,0},{4,6},{6,4},{1,3},{3,1},{5,7},{7,5},{8,10},{10,8},{12,... | collective-permute-start | bytes 129032 | tf_op jit(solution)/shard_map/ppermute | solution.py:340
  54.1 2.3 %collective-permute-done.1.other_ref = bf16[168,128]{1,0:T(8,128)(2,1)S(1)} collective-permute-done((bf16[168,128]{1,0:T(8,128)(2,1)S(1)}, bf16[168,128]{1,0:T(8,128)(2,1)S(1)}, u32[]{:S(2)}, u32[]{:S(2)}) %collective-permute-start.1) | collective-permute-done | bytes 43040 | tf_op jit(solution)/shard_map/ppermute | solution.py:340
  56.4 5.6 %collective-permute-start.2 = (bf16[168,128]{1,0:T(8,128)(2,1)S(1)}, bf16[168,128]{1,0:T(8,128)(2,1)S(1)}, u32[]{:S(2)}, u32[]{:S(2)}) collective-permute-start(bf16[168,128]{1,0:T(8,128)(2,1)S(1)} %shard_map.153.own_ref), channel_id=1, source_target_pairs={{0,6},{2,4},{4,2},{6,0},{1,7},{3,5},{5,3},{7,1},{8,14},{10,12},{12... | collective-permute-start | bytes 129032 | tf_op jit(solution)/shard_map/ppermute | solution.py:340
  62.0 2.9 %collective-permute-done.2.other_ref = bf16[168,128]{1,0:T(8,128)(2,1)S(1)} collective-permute-done((bf16[168,128]{1,0:T(8,128)(2,1)S(1)}, bf16[168,128]{1,0:T(8,128)(2,1)S(1)}, u32[]{:S(2)}, u32[]{:S(2)}) %collective-permute-start.2) | collective-permute-done | bytes 43040 | tf_op jit(solution)/shard_map/ppermute | solution.py:340
  64.9 0.7 shard_map.154
  65.6 3.4 %all-to-all-start.2 = ((bf16[4,168,128]{2,1,0:T(8,128)(2,1)}), bf16[4,168,128]{2,1,0:T(8,128)(2,1)S(1)}, u32[]{:S(2)}, u32[]{:S(2)}) async-start(bf16[4,168,128]{2,1,0:T(8,128)(2,1)} %shard_map.154), calls=%async_computation.2 | async-start | bytes 344064 | tf_op jit(solution)/shard_map/all_to_all | solution.py:447
  68.9 0.0 copy-done
  68.9 1.6 %shard_map.150 = bf16[384,384]{1,0:T(8,128)(2,1)} custom-call(f32[48,128]{1,0:T(8,128)S(1)} %get-tuple-element.8.refs_0_, bf16[448,384]{1,0:T(8,128)(2,1)S(1)} %bitcast.19), custom_call_target="tpu_custom_call" | custom-call | flops 1000000000 | bytes 663552 | tf_op jit(solution)/shard_map/pallas_call | solution.py:325
  70.6 4.5 %all-to-all-done.2 = bf16[4,168,128]{2,1,0:T(8,128)(2,1)S(1)} async-done(((bf16[4,168,128]{2,1,0:T(8,128)(2,1)}), bf16[4,168,128]{2,1,0:T(8,128)(2,1)S(1)}, u32[]{:S(2)}, u32[]{:S(2)}) %all-to-all-start.2) | async-done | bytes 172064 | tf_op jit(solution)/shard_map/all_to_all | solution.py:447
  75.1 4.9 %all-to-all-start.1 = ((bf16[24,16,384]{2,1,0:T(8,128)(2,1)}), bf16[24,16,384]{2,1,0:T(8,128)(2,1)S(1)}, u32[]{:S(2)}, u32[]{:S(2)}) async-start(bf16[24,16,384]{2,1,0:T(8,128)(2,1)} %bitcast.11), calls=%async_computation.1 | async-start | bytes 589824 | tf_op jit(solution)/shard_map/all_to_all | solution.py:444
  80.0 2.1 %all_gather.3.refs_0_ = bf16[8,168,128]{2,1,0:T(8,128)(2,1)S(1)} all-gather(bf16[4,168,128]{2,1,0:T(8,128)(2,1)S(1)} %all-to-all-done.2), channel_id=1, replica_groups=mesh['shard'=24,'x'=4,'y'=4,'core'=2] {'core'}, dimensions={0}, use_global_device_ids=true | all-gather | bytes 516096 | tf_op jit(solution)/shard_map/all_gather | solution.py:470
  82.1 0.0 copy-start.1
  82.1 0.0 copy-start.2
  82.1 0.0 copy-start.6
  82.1 0.0 copy-start.7
  82.1 0.9 shard_map.155
  83.0 0.0 copy-start.5
  83.0 11.3 %all-to-all-done.1 = bf16[24,16,384]{2,1,0:T(8,128)(2,1)S(1)} async-done(((bf16[24,16,384]{2,1,0:T(8,128)(2,1)}), bf16[24,16,384]{2,1,0:T(8,128)(2,1)S(1)}, u32[]{:S(2)}, u32[]{:S(2)}) %all-to-all-start.1) | async-done | bytes 294944 | tf_op jit(solution)/shard_map/all_to_all | solution.py:444
  94.4 0.0 copy-done.1
  94.4 0.0 copy-done.2
  94.4 0.0 copy-done.3
  94.4 0.0 copy-done.4
  94.4 0.0 copy-done.6
  94.4 0.0 copy-done.7
  94.4 0.0 copy-done.5
  94.4 5.2 %shard_map.151 = (bf16[9,64,128]{2,1,0:T(8,128)(2,1)}, f32[9,64,128]{2,1,0:T(8,128)}) custom-call(bf16[9,64,128]{2,1,0:T(8,128)(2,1)S(1)} %bitcast.21, bf16[9,64,128]{2,1,0:T(8,128)(2,1)S(1)} %bitcast.23, bf16[9,9,256]{2,1,0:T(8,128)(2,1)S(1)} %copy-done.3, bf16[256,128]{1,0:T(8,128)(2,1)S(1)} %copy-done.4, s32[1,256]{1,0:T(1,128)S(1)} %bitcast.25, ...), custom_call_target="tpu_custom_call" | custom-call | flops 5000000000 | bytes 1142272 | tf_op jit(solution)/shard_map/pallas_call | solution.py:325
  (4 shorter events, 0.0 us)
Async XLA Ops:
  46.3 3.1 %collective-permute-start = (bf16[168,128]{1,0:T(8,128)(2,1)S(1)}, bf16[168,128]{1,0:T(8,128)(2,1)S(1)}, u32[]{:S(2)}, u32[]{:S(2)}) collective-permute-start(bf16[168,128]{1,0:T(8,128)(2,1)S(1)} %get-tuple-element.12), channel_id=1, source_target_pairs={{0,1},{1,0},{2,3},{3,2},{4,5},{5,4},{6,7},{7,6},{8,9},{9,8},{10,11... | collective-permute-start | bytes 129032 | tf_op jit(solution)/shard_map/ppermute | solution.py:340
  49.4 19.5 %copy-start = (bf16[28,16,384]{2,1,0:T(8,128)(2,1)S(1)}, bf16[28,16,384]{2,1,0:T(8,128)(2,1)}, u32[]{:S(2)}) copy-start(bf16[28,16,384]{2,1,0:T(8,128)(2,1)} %param.25) | copy-start | bytes 1032196
  49.4 6.9 %collective-permute-start.1 = (bf16[168,128]{1,0:T(8,128)(2,1)S(1)}, bf16[168,128]{1,0:T(8,128)(2,1)S(1)}, u32[]{:S(2)}, u32[]{:S(2)}) collective-permute-start(bf16[168,128]{1,0:T(8,128)(2,1)S(1)} %shard_map.152.own_ref), channel_id=1, source_target_pairs={{0,2},{2,0},{4,6},{6,4},{1,3},{3,1},{5,7},{7,5},{8,10},{10,8},{12,... | collective-permute-start | bytes 129032 | tf_op jit(solution)/shard_map/ppermute | solution.py:340
  56.4 8.5 %collective-permute-start.2 = (bf16[168,128]{1,0:T(8,128)(2,1)S(1)}, bf16[168,128]{1,0:T(8,128)(2,1)S(1)}, u32[]{:S(2)}, u32[]{:S(2)}) collective-permute-start(bf16[168,128]{1,0:T(8,128)(2,1)S(1)} %shard_map.153.own_ref), channel_id=1, source_target_pairs={{0,6},{2,4},{4,2},{6,0},{1,7},{3,5},{5,3},{7,1},{8,14},{10,12},{12... | collective-permute-start | bytes 129032 | tf_op jit(solution)/shard_map/ppermute | solution.py:340
  65.6 9.5 %all-to-all-start.2 = ((bf16[4,168,128]{2,1,0:T(8,128)(2,1)}), bf16[4,168,128]{2,1,0:T(8,128)(2,1)S(1)}, u32[]{:S(2)}, u32[]{:S(2)}) async-start(bf16[4,168,128]{2,1,0:T(8,128)(2,1)} %shard_map.154), calls=%async_computation.2 | async-start | bytes 344064 | tf_op jit(solution)/shard_map/all_to_all | solution.py:447
  75.1 19.3 %all-to-all-start.1 = ((bf16[24,16,384]{2,1,0:T(8,128)(2,1)}), bf16[24,16,384]{2,1,0:T(8,128)(2,1)S(1)}, u32[]{:S(2)}, u32[]{:S(2)}) async-start(bf16[24,16,384]{2,1,0:T(8,128)(2,1)} %bitcast.11), calls=%async_computation.1 | async-start | bytes 589824 | tf_op jit(solution)/shard_map/all_to_all | solution.py:444
  82.1 12.3 %copy-start.1 = (bf16[64,9,128]{2,0,1:T(8,128)(2,1)S(1)}, bf16[64,9,128]{2,0,1:T(8,128)(2,1)}, u32[]{:S(2)}) copy-start(bf16[64,9,128]{2,0,1:T(8,128)(2,1)} %param.13) | copy-start | bytes 442372
  82.1 12.3 %copy-start.2 = (bf16[64,9,128]{2,0,1:T(8,128)(2,1)S(1)}, bf16[64,9,128]{2,0,1:T(8,128)(2,1)}, u32[]{:S(2)}) copy-start(bf16[64,9,128]{2,0,1:T(8,128)(2,1)} %param.14) | copy-start | bytes 442372
  82.1 12.3 %copy-start.3 = (bf16[9,9,256]{2,1,0:T(8,128)(2,1)S(1)}, bf16[9,9,256]{2,1,0:T(8,128)(2,1)}, u32[]{:S(2)}) copy-start(bf16[9,9,256]{2,1,0:T(8,128)(2,1)} %refs_2_.3) | copy-start | bytes 124420
  82.1 12.3 %copy-start.4 = (bf16[256,128]{1,0:T(8,128)(2,1)S(1)}, bf16[256,128]{1,0:T(8,128)(2,1)}, u32[]{:S(2)}) copy-start(bf16[256,128]{1,0:T(8,128)(2,1)} %refs_3_.3) | copy-start | bytes 196612
  82.1 12.3 %copy-start.6 = (s32[256]{0:T(256)S(1)}, s32[256]{0:T(256)}, u32[]{:S(2)}) copy-start(s32[256]{0:T(256)} %param.18) | copy-start | bytes 3076
  82.1 12.3 %copy-start.7 = (s32[256]{0:T(256)S(1)}, s32[256]{0:T(256)}, u32[]{:S(2)}) copy-start(s32[256]{0:T(256)} %param.19) | copy-start | bytes 3076
  83.0 11.4 %copy-start.5 = (s32[256]{0:T(256)S(1)}, s32[256]{0:T(256)}, u32[]{:S(2)}) copy-start(s32[256]{0:T(256)} %param.17) | copy-start | bytes 3076
